TPU v7x, 32 devices: a whole 2x2x4 slice. The times are simulated.
32 devices in a mesh: gy: 8 (over z, x), gx: 4 (over y, core).
Axes of the slice: x: 2, y: 2, z: 4, core: 2. Of those that a mesh axis runs over, the one named last changes fastest.
Arguments:
- ensemble: bfloat16 [32, 2, 512, 512], P(None, None, 'gy', 'gx'), may hold values from -1.1953125 to 1.1953125
- obs_cell: int32 [8, 4, 2048], P('gy', 'gx'), may hold values from 0 to 8191
- obs_level: int32 [8, 4, 2048], P('gy', 'gx'), may hold values from 0 to 1
- innovation: float32 [8, 4, 2048], P('gy', 'gx'), may hold values from -6 to 6
- obs_weight: float32 [8, 4, 2048], P('gy', 'gx'), may hold values from 0.5 to 4
Outputs:
- control: float32 [32, 2, 512, 512], P(None, None, 'gy', 'gx')
- increment: float32 [2, 512, 512], P(None, 'gy', 'gx')
Inputs may be any that keep to these rules, and one draw needn't show every extreme that they name: obs_cell holds row * 128 + column of the observation within its device's block of 64 x 128 cells.
All inputs are finite; a program needn't handle non-finite values.
Results may differ from a plain program's by a relative error of at most 0.0003.
Values sent between devices are 32-bit elements; how exact they have to be, the bound alone decides.
A program may use at most 128 MiB of HBM per device.

v0:
```python
import functools
import math
import jax
import jax.numpy as jnp
from jax import lax
from jax.experimental import pallas as pl
from jax.experimental.pallas import tpu as pltpu
from jax.sharding import PartitionSpec as P

SWEEPS = 4
KAPPA = 0.2
EPS = 1e-06
W = 2 * SWEEPS
HALF = 64
UNROLL = 4


def scatter(cell_ref, level_ref, inn_ref, wt_ref, g_ref, d_ref):
    levels, rows, cols = g_ref.shape
    cell = cell_ref[...]
    row = level_ref[...] * rows + cell // cols
    col = cell % cols
    n = cell.shape[1]
    hot = jnp.where(lax.broadcasted_iota(jnp.int32, (levels * rows, n), 0) == row, 1.0, 0.0).astype(jnp.bfloat16)
    at = lax.broadcasted_iota(jnp.int32, (cols, n), 0) == col
    wt = wt_ref[...]
    for ref, v in ((g_ref, wt * inn_ref[...]), (d_ref, wt)):
        hi = v.astype(jnp.bfloat16).astype(jnp.float32)
        lo = v - hi
        total = None
        for part in (hi, lo):
            sel = jnp.where(at, part, 0.0).astype(jnp.bfloat16)
            term = lax.dot_general(hot, sel, (((1,), (1,)), ((), ())), preferred_element_type=jnp.float32)
            total = term if total is None else total + term
        for l in range(levels):
            ref[l] = total[l * rows:(l + 1) * rows]


SIDES = [(-1, 0), (1, 0), (0, -1), (0, 1), (-1, -1), (-1, 1), (1, -1), (1, 1)]


def peer(dy, dx):
    ny, nx = lax.axis_size("gy"), lax.axis_size("gx")
    return {"gy": lax.rem(lax.axis_index("gy") + dy + ny, ny), "gx": lax.rem(lax.axis_index("gx") + dx + nx, nx)}


def meet():
    bar = pltpu.get_barrier_semaphore()
    for dy, dx in SIDES:
        pl.semaphore_signal(bar, inc=1, device_id=peer(dy, dx), device_id_type=pl.DeviceIdType.MESH)
    total = len(SIDES)
    for axis in ("gx", "gy"):
        n, me = lax.axis_size(axis), lax.axis_index(axis)
        total += n - 1
        for k in range(1, n):
            pl.semaphore_signal(bar, inc=1, device_id={axis: lax.rem(me + k, n)}, device_id_type=pl.DeviceIdType.MESH)
    pl.semaphore_wait(bar, total)


def send_all(pairs, ssem, rsem):
    copies = []
    for n, ((dy, dx), (src, dst)) in enumerate(zip(SIDES, pairs)):
        copies.append(pltpu.make_async_remote_copy(
            src_ref=src, dst_ref=dst, send_sem=ssem.at[n], recv_sem=rsem.at[n],
            device_id=peer(dy, dx), device_id_type=pl.DeviceIdType.MESH))
        copies[-1].start()
    return copies


def pack_state(g_ref, pe_ref, pw_ref):
    levels, rows, cols = g_ref.shape
    block = lax.broadcasted_iota(jnp.int32, (8, cols), 1) // W
    e = w = jnp.zeros((8, cols), jnp.float32)
    per = rows // 8
    for l in range(levels):
        for t in range(per):
            p = l * per + t
            x = pltpu.roll(g_ref[l, t * 8:t * 8 + 8], (p * W + W) % cols, 1)
            e = jnp.where(block == p, x, e)
            w = jnp.where(block == (p + 1) % (cols // W), x, w)
    pe_ref[...] = e
    pw_ref[...] = w


def unpack_state(g_ref, land_n, land_p, gm_ref, gs_ref):
    levels, rows, cols = g_ref.shape
    hr = rows + 2 * W
    per = rows // 8
    lane = lax.broadcasted_iota(jnp.int32, (8, cols), 1)
    block = lane // W
    gy, gx = lax.axis_index("gy"), lax.axis_index("gx")
    c = strip_col(lane, cols) + gx * cols
    cok = (lane % HALF < 6 * W) & (c >= 0) & (c < cols * lax.axis_size("gx"))
    for l in range(levels):
        for t in range(-1, per + 1):
            if t < 0:
                x, pe, pw, p = land_n[1, l], land_p[5], land_p[4], l * per + per - 1
            elif t == per:
                x, pe, pw, p = land_n[0, l], land_p[3], land_p[2], l * per
            else:
                x, pe, pw, p = g_ref[l, t * 8:t * 8 + 8], land_p[1], land_p[0], l * per + t
            r = lax.broadcasted_iota(jnp.int32, (8, cols), 0) + gy * rows + t * 8
            rok = (r >= 0) & (r < rows * lax.axis_size("gy"))
            x = jnp.where(rok, x, 0.0)
            z = jnp.where(block == p, pe, pw)
            z1 = pltpu.roll(z, (cols - p * W) % cols, 1)
            z2 = pltpu.roll(z, (cols - p * W + HALF) % cols, 1)
            own = jnp.where(lane < HALF, pltpu.roll(x, 4 * W, 1), pltpu.roll(x, HALF + 4 * W, 1))
            halo = jnp.where(lane < HALF, z1, z2)
            gs = jnp.where(lane % HALF < 2 * W, halo, own)
            at = slice((t + 1) * 8, (t + 2) * 8)
            gm_ref[l, at] = x
            gs_ref[l, at] = jnp.where(rok & cok, gs, 0.0)


def state_pairs(g_ref, pe_ref, pw_ref, land_n, land_p):
    rows = g_ref.shape[1]
    return [(g_ref.at[:, 0:W], land_n.at[0]), (g_ref.at[:, rows - W:rows], land_n.at[1])] + [
        (pw_ref if dx < 0 else pe_ref, land_p.at[n]) for n, (dy, dx) in enumerate(SIDES[2:])]


def state_scratch(levels, cols):
    f32 = jnp.float32
    dma = pltpu.SemaphoreType.DMA
    return [pltpu.VMEM((8, cols), f32), pltpu.VMEM((8, cols), f32), pltpu.VMEM((2, levels, W, cols), f32),
            pltpu.VMEM((6, 8, cols), f32), dma((8,)), dma((8,))]


def prep_kernel(ens_ref, cell_ref, level_ref, inn_ref, wt_ref, e_ref, s_ref, g_ref, d_ref, gm_ref, gs_ref,
                wm_ref, ws_ref, ec_ref, pe_ref, pw_ref, en_ref, pee_ref, pew_ref, pc_ref, es, er,
                gpe, gpw, gn, gp, ss, sr):
    members, levels, rows, cols = ens_ref.shape
    hr = rows + 2 * W
    per = rows // 8
    pairs = members // 16
    lane = lax.broadcasted_iota(jnp.int32, (8, cols), 1)
    block = lane // W
    nb = cols // W

    def convert(k, x):
        for l in range(levels):
            ec_ref[k * levels + l] = ens_ref[k, l].astype(jnp.float32)
        return x

    lax.fori_loop(0, members, convert, 0)

    def pack(t, x):
        at = pl.ds(pl.multiple_of(t * 8, 8), 8)
        for l in range(levels):
            for j in range(pairs):
                e = w = jnp.zeros((8, cols), jnp.float32)
                for b in range(2):
                    for i in range(8):
                        p = b * 8 + i
                        x8 = pltpu.roll(ec_ref[(16 * j + p) * levels + l, at, :], (p * W + W) % cols, 1)
                        e = jnp.where(block == p, x8, e)
                        w = jnp.where(block == (p + 1) % nb, x8, w)
                pe_ref[l * pairs + j, at, :] = e
                pw_ref[l * pairs + j, at, :] = w
        return x

    lax.fori_loop(0, per, pack, 0)
    meet()
    top, bottom = slice(0, W), slice(rows - W, rows)
    jobs = [(ec_ref.at[:, top], en_ref.at[0]), (ec_ref.at[:, bottom], en_ref.at[1]), (pw_ref, pew_ref), (pe_ref, pee_ref)]
    for n, (dy, dx) in enumerate(SIDES[4:]):
        src = pw_ref if dx < 0 else pe_ref
        jobs.append((src.at[:, top if dy < 0 else bottom], pc_ref.at[n]))
    ecopies = send_all(jobs, es, er)
    scatter(cell_ref, level_ref, inn_ref, wt_ref, g_ref, d_ref)
    pack_state(g_ref, gpe, gpw)
    gcopies = send_all(state_pairs(g_ref, gpe, gpw, gn, gp), ss, sr)

    def center(f, x):
        e_ref[pl.ds(pl.multiple_of(f * hr + W, 8), rows), :] = ec_ref[f]
        return x

    lax.fori_loop(0, members * levels, center, 0)
    weight_kernel(wm_ref, ws_ref, cols=cols)
    for c in ecopies:
        c.wait_recv()

    def edges(f, x):
        e_ref[pl.ds(pl.multiple_of(f * hr, 8), W), :] = en_ref[1, f]
        e_ref[pl.ds(pl.multiple_of(f * hr + W + rows, 8), W), :] = en_ref[0, f]
        return x

    lax.fori_loop(0, members * levels, edges, 0)

    def strip_tile(lj, i, l, j, row, pe, pw):
        a = e_ref[pl.ds(pl.multiple_of(((16 * j + i) * levels + l) * hr + row, 8), 8), :]
        b = e_ref[pl.ds(pl.multiple_of(((16 * j + 8 + i) * levels + l) * hr + row, 8), 8), :]
        own = jnp.where(lane < HALF, pltpu.roll(a, 4 * W, 1), pltpu.roll(b, HALF + 4 * W, 1))
        z = pltpu.roll(jnp.where(block % 8 == i, pe, pw), (cols - i * W) % cols, 1)
        s_ref[pl.ds(pl.multiple_of((lj * 8 + i) * hr + row, 8), 8), :] = jnp.where(lane % HALF < 2 * W, z, own)

    for l in range(levels):
        for j in range(pairs):
            lj = l * pairs + j

            def mid(t, x):
                at = pl.ds(pl.multiple_of(t * 8, 8), 8)
                pe, pw = pee_ref[lj, at, :], pew_ref[lj, at, :]
                for i in range(8):
                    strip_tile(lj, i, l, j, W + t * 8, pe, pw)
                return x

            lax.fori_loop(0, per, mid, 0)
            for i in range(8):
                strip_tile(lj, i, l, j, 0, pc_ref[3, lj], pc_ref[2, lj])
                strip_tile(lj, i, l, j, W + rows, pc_ref[1, lj], pc_ref[0, lj])
    for c in gcopies:
        c.wait_recv()
    unpack_state(g_ref, gn, gp, gm_ref, gs_ref)
    for c in ecopies + gcopies:
        c.wait_send()


def next_kernel(y_ref, d_ref, gm_ref, gs_ref, g_ref, gpe, gpw, gn, gp, ss, sr):
    g_ref[...] = d_ref[...] * y_ref[...]
    pack_state(g_ref, gpe, gpw)
    copies = send_all(state_pairs(g_ref, gpe, gpw, gn, gp), ss, sr)
    for c in copies:
        c.wait_recv()
    unpack_state(g_ref, gn, gp, gm_ref, gs_ref)
    for c in copies:
        c.wait_send()


def out_kernel(m_ref, p0_ref, s0_ref, p1_ref, s1_ref, y0_ref, y1_ref, c_ref, inc_ref):
    levels, rows, cols = y0_ref.shape
    groups = p0_ref.shape[0] // levels
    pairs = groups // 2
    m = jnp.sum(m_ref[...], axis=1, keepdims=True)
    m = [m[k:k + 1] for k in range(4)]
    bn2 = m[0] + EPS
    c = (EPS - m[1]) / bn2
    alpha1 = (m[0] + m[1]) / bn2
    r2 = jnp.maximum((c * c * m[0] + 2.0 * c * m[1] + m[2]) / bn2, 0.0)
    rho = (c * c * m[1] + 2.0 * c * m[2] + m[3]) / bn2
    b2 = r2 + EPS
    alpha2 = (r2 + rho) / b2
    det = alpha1 * alpha2 - b2
    ca = jnp.broadcast_to((alpha2 - c) / det, (8, cols))
    cb = jnp.broadcast_to(-1.0 / det, (8, cols))
    for l in range(levels):
        for t in range(rows // 8):
            at = slice(t * 8, t * 8 + 8)
            inc_ref[l, at] = ca * y0_ref[l, at] + cb * y1_ref[l, at]
    lane = lax.broadcasted_iota(jnp.int32, (8, cols), 1)
    edge = (lane < W) | (lane >= cols - W)
    for l in range(levels):
        for j in range(pairs):
            def row(r, x):
                s = ca * s0_ref[l * pairs + j, W + r] + cb * s1_ref[l * pairs + j, W + r]
                for b in range(2):
                    g = l * groups + 2 * j + b
                    main = ca * p0_ref[g, W + r] + cb * p1_ref[g, W + r]
                    v = jnp.where(edge, pltpu.roll(s, (2 * cols - 4 * W - b * HALF) % cols, 1), main)
                    c_ref[pl.ds(((2 * j + b) * 8 * levels + l) * rows + r, 8, stride=levels * rows), :] = v
                return x

            lax.fori_loop(0, rows, row, 0, unroll=8)


def strip_col(lane, cols):
    lane = lane % HALF
    return jnp.where(lane < W, lane - W, jnp.where(lane < 2 * W, lane - W + cols,
                     jnp.where(lane < 4 * W, lane - 4 * W + cols, lane - 4 * W)))


def weight_kernel(wm_ref, ws_ref, *, cols):
    i = lax.broadcasted_iota(jnp.int32, (cols, cols), 0)
    j = lax.broadcasted_iota(jnp.int32, (cols, cols), 1)
    near = jnp.abs(i - j) <= 1
    gx = lax.axis_index("gx")

    def real(lane):
        c = strip_col(lane, cols) + gx * cols
        return (lane % HALF < 6 * W) & (c >= 0) & (c < cols * lax.axis_size("gx"))

    si, sj = strip_col(i, cols), strip_col(j, cols)
    same = ((i < HALF) == (j < HALF)) & (jnp.abs(si - sj) <= 1)

    for ref, ok in ((wm_ref, near), (ws_ref, same & real(i) & real(j))):
        one = jnp.where(ok, 1.0, 0.0).astype(jnp.bfloat16)
        power = one
        for s in range(1, SWEEPS + 1):
            if s > 1:
                power = jnp.dot(power, one, preferred_element_type=jnp.float32).astype(jnp.bfloat16)
            scaled = (power.astype(jnp.float32) * float(math.comb(SWEEPS, s))).astype(jnp.bfloat16)
            ref[0:cols, (s - 1) * cols:s * cols] = scaled
            ref[cols:2 * cols, (s - 1) * cols:s * cols] = scaled


def g_kernel(e_ref, s_ref, g_ref, gs_ref, wm_ref, ws_ref, p_ref, ps_ref, y_ref, km_ref, ym_ref, yst_ref,
             u_ref, lhs_ref, f_ref, *, members, levels, rows, cols):
    hr = rows + 2 * W
    groups = members // 8
    pairs = groups // 2
    count = groups + pairs
    scale = KAPPA ** SWEEPS
    gy = lax.axis_index("gy")
    rr = lax.broadcasted_iota(jnp.int32, (hr, cols), 0) + gy * rows - W
    km_ref[...] = jnp.where((rr >= 0) & (rr < rows * lax.axis_size("gy")), 1.0, 0.0)

    def e_row(l, m, r):
        return e_ref[pl.ds(((m * 8) * levels + l) * hr + r, 8, stride=levels * hr), :]

    def s_row(l, j, r):
        return s_ref[pl.ds(((l * pairs + j) * 8) * hr + r, 8, stride=hr), :]

    def ek_row(l, c, r):
        return e_row(l, c, r) if c < groups else s_row(l, c - groups, r)

    def split(c, r, u):
        hi = u.astype(jnp.bfloat16)
        lo = (u - hi.astype(jnp.float32)).astype(jnp.bfloat16)
        return hi, lo

    def products(lo_row, n):
        for c in range(count):
            w = wm_ref if c < groups else ws_ref
            f_ref[c, pl.ds(lo_row * 8, n * 8), :] = jnp.dot(
                lhs_ref[c, pl.ds(lo_row * 8, n * 8), :], w[...], preferred_element_type=jnp.float32)

    def sweep_all(state, vals, r):
        new = []
        for s in range(SWEEPS):
            o = jnp.maximum(r - s - 1, 0)
            km = km_ref[pl.ds(o, 1), :]
            out = []
            at = pl.ds(pl.multiple_of(o * 8, 8), 8)
            for c, u in enumerate(vals):
                older, prev = state[s][c]
                out.append(km * (older + u) + f_ref[c, at, s * cols:(s + 1) * cols])
                new.append((prev, u))
            vals = out
        return [new[s * count:(s + 1) * count] for s in range(SWEEPS)], [v * scale for v in vals]

    zero = km_ref[0:8, :] * 0.0
    start = [[(zero, zero)] * count for _ in range(SWEEPS)]
    step = hr

    def store_lhs(c, r, us):
        his, los = zip(*[split(c, r, u) for u in us])
        at = pl.ds(pl.multiple_of(r * 8, 16), 16)
        lhs_ref[c, at, 0:cols] = jnp.concatenate(his, axis=0)
        lhs_ref[c, at, cols:2 * cols] = jnp.concatenate(los, axis=0)

    for l in range(levels):
        def fill(i, carry):
            r = i * 2
            for c in range(count):
                us = []
                for k in range(2):
                    g = (g_ref if c < groups else gs_ref)[l, pl.ds(r + k, 1), :]
                    u = ek_row(l, c, r + k) * g
                    u_ref[c, r + k] = u
                    us.append(u)
                store_lhs(c, r, us)
            return carry

        lax.fori_loop(0, hr // 2, fill, 0, unroll=2)
        products(0, step)

        def first(r, state):
            state, vals = sweep_all(state, [u_ref[c, r] for c in range(count)], r)
            o = jnp.maximum(r - SWEEPS, 0)
            for m in range(groups):
                p_ref[l * groups + m, o] = vals[m]
            for j in range(pairs):
                ps_ref[l * pairs + j, o] = vals[groups + j]
            return state

        lax.fori_loop(0, hr, first, start, unroll=UNROLL)

        def refill(i, carry):
            r = i * 2
            for c in range(count):
                p = p_ref.at[l * groups + c] if c < groups else ps_ref.at[l * pairs + c - groups]
                store_lhs(c, r, [p[r], p[r + 1]])
            return carry

        lax.fori_loop(SWEEPS // 2, (hr - SWEEPS) // 2, refill, 0, unroll=2)
        products(0, step)

        def second(r, state):
            vals = [p_ref[l * groups + m, r] for m in range(groups)] + [ps_ref[l * pairs + j, r] for j in range(pairs)]
            state, vals = sweep_all(state, vals, r)
            o = jnp.maximum(r - SWEEPS, 0)
            acc = None
            for m in range(groups):
                t = vals[m] * e_row(l, m, o)
                acc = t if acc is None else acc + t
            ym_ref[l, o] = acc
            acc = None
            for j in range(pairs):
                t = vals[groups + j] * s_row(l, j, o)
                acc = t if acc is None else acc + t
            yst_ref[l, o] = acc
            return state

        lax.fori_loop(SWEEPS, hr - SWEEPS, second, start, unroll=UNROLL)
    lane = lax.broadcasted_iota(jnp.int32, (rows, cols), 1)
    for l in range(levels):
        main = jnp.sum(ym_ref[l, W:W + rows], axis=1)
        st = jnp.sum(yst_ref[l, W:W + rows], axis=1)
        st = st + pltpu.roll(st, HALF, 1)
        y_ref[l] = jnp.where((lane < W) | (lane >= cols - W), pltpu.roll(st, cols - 4 * W, 1), main)


def sum_kernel(x_ref, o_ref, mid_ref, ra_ref, rb_ref, sa, qa, sb, qb):
    nx, ny = lax.axis_size("gx"), lax.axis_size("gy")
    mx, my = lax.axis_index("gx"), lax.axis_index("gy")
    def stage(axis, n, me, src, land, ssem, rsem):
        copies = []
        for k in range(1, n):
            copies.append(pltpu.make_async_remote_copy(
                src_ref=src, dst_ref=land.at[k - 1], send_sem=ssem.at[k - 1], recv_sem=rsem.at[k - 1],
                device_id={axis: lax.rem(me + k, n)}, device_id_type=pl.DeviceIdType.MESH))
            copies[-1].start()
        for c in copies:
            c.wait_recv()
        total = src[...]
        for k in range(n - 1):
            total = total + land[k]
        return copies, total

    ca, total = stage("gx", nx, mx, x_ref, ra_ref, sa, qa)
    mid_ref[...] = total
    cb, total = stage("gy", ny, my, mid_ref, rb_ref, sb, qb)
    o_ref[...] = total
    for c in ca + cb:
        c.wait_send()


def whole_kernel(ens_ref, cell_ref, level_ref, inn_ref, wt_ref, c_ref, inc_ref,
                 e_ref, s_ref, g_ref, d_ref, gm_ref, gs_ref, wm_ref, ws_ref, p0, s0, y0, p1, s1, y1, g1_ref,
                 x_ref, m_ref, *rest):
    members, levels, rows, cols = ens_ref.shape
    dims = dict(members=members, levels=levels, rows=rows, cols=cols)
    ens_bufs, first_bufs, second_bufs, work, sum_bufs = rest[:9], rest[9:15], rest[15:21], rest[21:27], rest[27:]
    prep_kernel(ens_ref, cell_ref, level_ref, inn_ref, wt_ref, e_ref, s_ref, g_ref, d_ref, gm_ref, gs_ref,
                wm_ref, ws_ref, *ens_bufs, *first_bufs)
    g_kernel(e_ref, s_ref, gm_ref, gs_ref, wm_ref, ws_ref, p0, s0, y0, *work, **dims)
    next_kernel(y0, d_ref, gm_ref, gs_ref, g1_ref, *second_bufs)
    g_kernel(e_ref, s_ref, gm_ref, gs_ref, wm_ref, ws_ref, p1, s1, y1, *work, **dims)
    x_ref[...] = jnp.zeros_like(x_ref)
    for k, (a, b) in enumerate(((g_ref, y0), (g1_ref, y0), (g1_ref, y1), (None, y1))):
        v = d_ref[...] * y1[...] * y1[...] if a is None else a[...] * b[...]
        x_ref[k:k + 1, :] = jnp.sum(v.reshape(levels * rows, cols), axis=0, keepdims=True)
    sum_kernel(x_ref, m_ref, *sum_bufs)
    out_kernel(m_ref, p0, s0, p1, s1, y0, y1, c_ref, inc_ref)


def on_device(ensemble, obs_cell, obs_level, innovation, obs_weight):
    members, levels, rows, cols = ensemble.shape
    hr = rows + 2 * W
    f = members * levels
    groups = members // 8
    pairs = groups // 2
    count = groups + pairs
    q = levels * pairs
    nx, ny = lax.axis_size("gx"), lax.axis_size("gy")
    f32 = jnp.float32
    vm = pl.BlockSpec(memory_space=pltpu.VMEM)
    dma = pltpu.SemaphoreType.DMA
    v = lambda *s: pltpu.VMEM(s, f32)
    flat = lambda a: a.reshape(1, -1)
    image = [v(levels * groups, hr, 8, cols), v(levels * pairs, hr, 8, cols), v(levels, rows, cols)]
    weights = [pltpu.VMEM((2 * cols, SWEEPS * cols), jnp.bfloat16)] * 2
    control, increment = pl.pallas_call(
        whole_kernel,
        out_shape=(jax.ShapeDtypeStruct((f * rows, cols), f32), jax.ShapeDtypeStruct((levels, rows, cols), f32)),
        in_specs=[vm] * 5,
        out_specs=(vm, vm),
        scratch_shapes=[v(f * hr, cols), v(q * 8 * hr, cols), v(levels, rows, cols), v(levels, rows, cols),
                        v(levels, hr, cols), v(levels, hr, cols)] + weights + image + image
        + [v(levels, rows, cols), v(8, cols), v(8, cols)]
        + [v(f, rows, cols), v(q, rows, cols), v(q, rows, cols), v(2, f, W, cols), v(q, rows, cols), v(q, rows, cols),
           v(4, q, W, cols), dma((8,)), dma((8,))]
        + state_scratch(levels, cols) + state_scratch(levels, cols)
        + [v(hr, cols), v(levels, hr, 8, cols), v(levels, hr, 8, cols), v(count, hr, 8, cols),
           pltpu.VMEM((count, hr * 8, 2 * cols), jnp.bfloat16), v(count, hr * 8, SWEEPS * cols)]
        + [v(8, cols), v(nx - 1, 8, cols), v(ny - 1, 8, cols), dma((nx - 1,)), dma((nx - 1,)), dma((ny - 1,)), dma((ny - 1,))],
        compiler_params=pltpu.CompilerParams(collective_id=0, has_side_effects=True, vmem_limit_bytes=64000000),
    )(ensemble, flat(obs_cell), flat(obs_level), flat(innovation), flat(obs_weight))
    return (control.reshape(members, levels, rows, cols), increment)


def solution(mesh):
    return jax.shard_map(
        on_device,
        mesh=mesh,
        in_specs=(
            P(None, None, "gy", "gx"),
            P("gy", "gx", None),
            P("gy", "gx", None),
            P("gy", "gx", None),
            P("gy", "gx", None),
        ),
        out_specs=(P(None, None, "gy", "gx"), P(None, "gy", "gx")),
        check_vma=False,
    )
```

profile of v0, /device:TPU:0, one launch (start us, length us, event | category | flops | bytes accessed | tf_op | source)
XLA Modules:
  0.0 81.1 jit_solution(14068196049407560372)
XLA Ops:
  0.6 76.6 %shard_map.68 = (f32[4096,128]{1,0:T(8,128)}, f32[2,64,128]{2,1,0:T(8,128)}) custom-call(bf16[32,2,64,128]{3,2,1,0:T(8,128)(2,1)} %ens_ref.1, s32[1,2048]{1,0:T(1,128)} %bitcast.6, s32[1,2048]{1,0:T(1,128)} %bitcast.7, f32[1,2048]{1,0:T(1,128)} %bitcast.8, f32[1,2048]{1,0:T(1,128)} %bitcast.9), custom_call_target="tpu_custom_call" | custom-call | tf_op jit(solution)/shard_map/pallas_call | solution.py:473
  77.2 0.0 copy-start
  77.2 3.2 %copy.9 = f32[32,2,64,128]{3,2,1,0:T(8,128)} copy(f32[32,2,64,128]{3,2,1,0:T(8,128)} %bitcast.5) | data formatting | bytes 4194304
  80.4 0.0 copy-done
  80.4 0.6 copy.10
Async XLA Ops:
  77.2 3.2 %copy-start = (f32[2,64,128]{2,1,0:T(8,128)S(1)}, f32[2,64,128]{2,1,0:T(8,128)}, u32[]{:S(2)}) copy-start(f32[2,64,128]{2,1,0:T(8,128)} %get-tuple-element.9) | copy-start | bytes 196612
where the time goes:
time: 81.2 us; the launch traced here: 81.1 us
  Pallas kernels  76.6 us (94%)
  local copies, waits for them, and re-layouts  3.82 us (5%)
    pallas_call x1, Pallas kernels, on_device(): pl.pallas_call(whole_kernel, out_shape=(jax.ShapeDtypeStruct((f * rows, c...  76.6 us
    unnamed x4, local copies, waits for them, and re-layouts  3.82 us

commit v1 on v0

v1 whole, which is shorter than its diff:
```python
import math
import jax
import jax.numpy as jnp
from jax import lax
from jax.experimental import pallas as pl
from jax.experimental.pallas import tpu as pltpu
from jax.sharding import PartitionSpec as P

SWEEPS = 4
KAPPA = 0.2
EPS = 1e-06
D = SWEEPS
BASE = 8
LANES = 128
SIDES = [(-1, 0), (1, 0), (0, -1), (0, 1), (-1, -1), (-1, 1), (1, -1), (1, 1)]
N_, S_, W_, E_, NW, NE, SW, SE = range(8)
BACK = [S_, N_, E_, W_, SE, SW, NE, NW]
MESH = pl.DeviceIdType.MESH
f32, bf16 = jnp.float32, jnp.bfloat16


class Dims:
    def __init__(self, members, levels, rows, cols):
        self.members, self.levels, self.rows, self.cols = members, levels, rows, cols
        self.fields = members * levels
        self.halves = LANES // self.fields
        assert self.halves == 2 and cols == LANES and levels * rows == LANES
        self.r = rows // self.halves
        self.rr = self.r + 2 * D
        self.groups = (cols + 2 * D) // 8
        self.st = -(-(cols + 2 * D) // 16) * 16
        self.size = BASE + self.rr * self.st + 8


def peer(dy, dx):
    ny, nx = lax.axis_size("gy"), lax.axis_size("gx")
    return {"gy": lax.rem(lax.axis_index("gy") + dy + ny, ny), "gx": lax.rem(lax.axis_index("gx") + dx + nx, nx)}


def meet_signal():
    bar = pltpu.get_barrier_semaphore()
    for dy, dx in SIDES:
        pl.semaphore_signal(bar, inc=1, device_id=peer(dy, dx), device_id_type=MESH)
    for axis in ("gx", "gy"):
        n, me = lax.axis_size(axis), lax.axis_index(axis)
        for k in range(1, n):
            pl.semaphore_signal(bar, inc=1, device_id={axis: lax.rem(me + k, n)}, device_id_type=MESH)


def meet_wait():
    total = len(SIDES) + lax.axis_size("gx") + lax.axis_size("gy") - 2
    pl.semaphore_wait(pltpu.get_barrier_semaphore(), total)


def send(n, src, dst, ssem, rsem):
    dy, dx = SIDES[n]
    c = pltpu.make_async_remote_copy(src_ref=src, dst_ref=dst, send_sem=ssem.at[n], recv_sem=rsem.at[n],
                                     device_id=peer(dy, dx), device_id_type=MESH)
    c.start()
    return c


def lane_iota(rows):
    return lax.broadcasted_iota(jnp.int32, (rows, LANES), 1)


def flip(x):
    return pltpu.roll(x, LANES // 2, 1)


def scatter(d, cell_ref, level_ref, inn_ref, wt_ref, go, do):
    cell = cell_ref[...]
    row = level_ref[...] * d.rows + cell // d.cols
    col = cell % d.cols
    n = cell.shape[1]
    hot = jnp.where(lax.broadcasted_iota(jnp.int32, (d.levels * d.rows, n), 0) == row, 1.0, 0.0).astype(bf16)
    at = lax.broadcasted_iota(jnp.int32, (d.cols, n), 0) == col
    wt = wt_ref[...]
    for ref, v in ((go, wt * inn_ref[...]), (do, wt)):
        hi = v.astype(bf16).astype(f32)
        total = None
        for part in (hi, v - hi):
            sel = jnp.where(at, part, 0.0).astype(bf16)
            term = lax.dot_general(sel, hot, (((1,), (1,)), ((), ())), preferred_element_type=f32)
            total = term if total is None else total + term
        ref[D:D + d.cols, :] = total
        ref[0:D, :] = jnp.zeros((D, LANES), f32)
        ref[D + d.cols:d.st, :] = jnp.zeros((d.st - D - d.cols, LANES), f32)


def row_masks(d, rows):
    rowl = lane_iota(rows) % d.rows
    return rowl < D, rowl >= d.rows - D, (rowl >= d.r - D) & (rowl < d.r + D)


def exchange_buffers(n):
    v = lambda *s: pltpu.VMEM((n,) + s, f32)
    one = [v(3, 8, LANES)] * 2 + [v(2, 8, LANES)] * 2 + [v(8, LANES)] * 4
    dma = pltpu.SemaphoreType.DMA
    return one + one + [dma((8,)), dma((8,))]


def exchange(d, pairs, bufs):
    out, land, ssem, rsem = bufs[:8], bufs[8:16], bufs[16], bufs[17]
    lo, hi, mid = row_masks(d, 8)
    last = d.groups - 1
    at = lambda g: slice(g * 8, g * 8 + 8)
    for a, (yo, yr) in enumerate(pairs):
        packs = [[None] * 3, [None] * 3]
        for g in range(d.groups):
            own, ring = yo[at(g), :], yr[at(g), :]
            own = own + jnp.where(mid, ring, 0.0)
            yo[at(g), :] = own
            for k in range(2):
                v = jnp.where(lo, own if k == 0 else ring, jnp.where(hi, ring if k == 0 else own, 0.0))
                if g == 0:
                    out[NW + 2 * k][a] = v
                if g == last:
                    out[NE + 2 * k][a] = v
                v = pltpu.roll(v, D + 8 * (g % 8), 1)
                packs[k][g // 8] = v if packs[k][g // 8] is None else packs[k][g // 8] + v
            if g == 0 or g == last:
                m = out[W_ if g == 0 else E_]
                m[a, 0] = own
                m[a, 1] = ring
        for k in range(2):
            for j in range(3):
                out[k][a, j] = packs[k][j]
    copies = [send(n, out[n], land[BACK[n]], ssem, rsem) for n in (N_, S_, W_, E_, NW, NE, SW, SE)]
    for c in copies:
        c.wait_recv()
    for a, (yo, yr) in enumerate(pairs):
        for g in range(d.groups):
            own, ring = yo[at(g), :], yr[at(g), :]
            shift = (LANES - D - 8 * (g % 8)) % LANES
            north = pltpu.roll(land[N_][a, g // 8], shift, 1)
            south = pltpu.roll(land[S_][a, g // 8], shift, 1)
            if g == 0:
                north, south = north + land[NW][a], south + land[SW][a]
            if g == last:
                north, south = north + land[NE][a], south + land[SE][a]
            if g == 0 or g == last:
                m = land[W_ if g == 0 else E_]
                own, ring = own + m[a, 0], ring + m[a, 1]
            own = own + jnp.where(lo, north, jnp.where(hi, south, 0.0))
            ring = ring + jnp.where(hi, north, jnp.where(lo, south, 0.0))
            yo[at(g), :] = own
            yr[at(g), :] = jnp.where(mid, own, ring)
    return copies


def build_selectors(d, sel, bsel):
    def code(x_iota, l_iota):
        level = x_iota // d.rows
        half = l_iota // d.fields
        base = lax.rem(lax.rem(x_iota, d.rows) - d.r * half + d.rows, d.rows)
        return jnp.where(lax.rem(l_iota, d.levels) == level, base, -1)

    a = lax.broadcasted_iota(jnp.int32, (LANES, LANES), 0)
    b = lax.broadcasted_iota(jnp.int32, (LANES, LANES), 1)
    for_sel, for_bsel = code(a, b), code(b, a)

    def fill(q, x):
        for s in range(2):
            i = q * 2 + s
            want = lax.rem(i - D + d.rows, d.rows)
            one = jnp.where(for_sel == want, 1.0, 0.0).astype(bf16)
            two = jnp.where(for_bsel == want, 1.0, 0.0).astype(bf16)
            for k in range(2):
                sel[q, k * LANES:(k + 1) * LANES, s * LANES:(s + 1) * LANES] = one
                bsel[pl.ds(pl.multiple_of(i * 256 + k * LANES, LANES), LANES), :] = two
        return x

    lax.fori_loop(0, d.rr // 2, fill, 0)


def split(x):
    hi = x.astype(bf16)
    return hi, (x - hi.astype(f32)).astype(bf16)


def expand(d, go, gr, sel, et, u):
    def wide(ref):
        hi, lo = split(ref[...])
        return jnp.concatenate([hi, lo], axis=1)

    own, ring = wide(go), wide(gr)
    pairs = d.rr // 2
    edge = D // 2
    for q in range(pairs):
        x = ring if q < edge or q >= pairs - edge else own
        g2 = jnp.dot(x, sel[q], preferred_element_type=f32)
        for s in range(2):
            at = BASE + (2 * q + s) * d.st
            n = d.groups * 8
            u[at:at + n, :] = et[at:at + n, :] * g2[0:n, s * LANES:(s + 1) * LANES]


def stencil(d, src, p, lo, hi, use):
    def ld(r, o):
        return src[pl.ds(p + (BASE + (r + D) * d.st + o), 8), :]

    n, c = ld(lo - 1, 0), ld(lo, 0)
    for r in range(lo, hi):
        s = ld(r + 1, 0)
        use(r, (n + s) + (c + (ld(r, -1) + ld(r, 1))))
        n, c = c, s


def sweep(d, src, dst, ext, masks):
    cm, rt, rb = masks

    def body(g, x):
        p = pl.multiple_of(g * 8, 8)
        m = cm[pl.ds(p, 8), :]
        mt, mb = m * rt[...], m * rb[...]

        def use(r, v):
            dst[pl.ds(p + (BASE + (r + D) * d.st), 8), :] = v * (mt if r < 0 else mb if r >= d.r else m)

        stencil(d, src, p, -ext, d.r + ext, use)
        return x

    lax.fori_loop(0, d.groups, body, 0)


def half_filter(d, src, bufs, pad, po, masks):
    a1, a2, a3 = bufs
    sweep(d, src, a1, 3, masks)
    sweep(d, a1, a2, 2, masks)
    sweep(d, a2, a3, 1, masks)

    def body(g, x):
        p = g * 8 + D

        def use(r, v):
            pad[pl.ds(p + (BASE + (r + D) * d.st), 8), :] = v
            po[r, pl.ds(pl.multiple_of(g * 8, 8), 8), :] = v

        stencil(d, a3, p, 0, d.r, use)
        return x

    lax.fori_loop(0, d.cols // 8, body, 0)


def back_filter(d, pad, bufs, et, lhs, masks):
    b1, b2, b3 = bufs
    sweep(d, pad, b1, 1, masks)
    sweep(d, b1, b2, 2, masks)
    sweep(d, b2, b3, 3, masks)
    zero = jnp.zeros((8, LANES), f32)

    def pair(p, q, both):
        def ld(r, o):
            return b3[pl.ds(p + (BASE + (r + D) * d.st + o), 8), :]

        n = [None, None]
        c = [ld(-D, 0), ld(-D, 8) if both else None]
        for r in range(-D, d.r + D):
            ts = []
            for k in range(2 if both else 1):
                o = 8 * k
                v = c[k] + (ld(r, o - 1) + ld(r, o + 1))
                s = None
                if r < d.r + D - 1:
                    s = ld(r + 1, o)
                    v = v + s
                if r > -D:
                    v = v + n[k]
                n[k], c[k] = c[k], s
                ts.append(v * et[pl.ds(p + (BASE + (r + D) * d.st + o), 8), :])
            if not both:
                ts.append(zero)
            hi, lo = split(jnp.concatenate(ts, axis=0))
            at = (r + D) * 2 * LANES
            lhs[pl.ds(q, 16), at:at + LANES] = hi
            lhs[pl.ds(q, 16), at + LANES:at + 2 * LANES] = lo

    def body(g, x):
        p = pl.multiple_of(g * 16, 16)
        pair(p, p, True)
        return x

    lax.fori_loop(0, d.groups // 2, body, 0)
    pair(d.groups // 2 * 16, d.groups // 2 * 16, False)


def reduce_members(d, lhs, bsel, yo, yr):
    k0, k1, k2 = D * 2 * LANES, (D + d.r) * 2 * LANES, d.rr * 2 * LANES
    scale = KAPPA ** (2 * SWEEPS)
    dot = lambda a, b: jnp.dot(lhs[:, a:b], bsel[a:b, :], preferred_element_type=f32)
    yo[...] = dot(k0, k1) * scale
    yr[...] = (dot(0, k0) + dot(k1, k2)) * scale


def all_sum(x_ref, o_ref, mid_ref, ra_ref, rb_ref, sa, qa, sb, qb):
    nx, ny = lax.axis_size("gx"), lax.axis_size("gy")
    mx, my = lax.axis_index("gx"), lax.axis_index("gy")

    def stage(axis, n, me, src, land, ssem, rsem):
        copies = []
        for k in range(1, n):
            copies.append(pltpu.make_async_remote_copy(
                src_ref=src, dst_ref=land.at[k - 1], send_sem=ssem.at[k - 1], recv_sem=rsem.at[k - 1],
                device_id={axis: lax.rem(me + k, n)}, device_id_type=MESH))
            copies[-1].start()
        for c in copies:
            c.wait_recv()
        total = src[...]
        for k in range(n - 1):
            total = total + land[k]
        return copies, total

    ca, total = stage("gx", nx, mx, x_ref, ra_ref, sa, qa)
    mid_ref[...] = total
    cb, total = stage("gy", ny, my, mid_ref, rb_ref, sb, qb)
    o_ref[...] = total
    for c in ca + cb:
        c.wait_send()


def ens_send_rows(d, et, hn, hs):
    lane = lane_iota(d.cols)
    low = lane < LANES // 2
    at = lambda r: et[BASE + (r + D) * d.st + D:BASE + (r + D) * d.st + D + d.cols, :]
    for i in range(2):
        hn[i] = jnp.where(low, at(i), flip(at(i + 2)))
        hs[i] = jnp.where(low, flip(at(d.r - 2 + i)), at(d.r - 4 + i))


def main_kernel(d, ens, cell, level, inn, wt, p0_out, p1_out, y0_out, y1_out, m_out, *refs):
    refs = list(refs)
    take = lambda n: [refs.pop(0) for _ in range(n)]
    ec, et, u, a1, a2, a3, pad, b1, b2, b3 = take(10)
    sel, bsel, lhs, po0, po1 = take(5)
    cm, rt, rb = masks = take(3)
    hn, hs, hw, he, ln, ls, lw, le, lnw, lne, lsw, lse, esem, rsem = take(14)
    go, gr, do, dr, g1o, g1r, y0o, y0r, y1o, y1r = take(10)
    ex0, ex1, ex2 = take(18), take(18), take(18)
    x_ref, mid_ref, ra_ref, rb_ref, sa, qa, sb, qb = take(8)
    osem = refs.pop(0)
    es = d.rows + 1
    gy, gx = lax.axis_index("gy"), lax.axis_index("gx")
    ny, nx = lax.axis_size("gy"), lax.axis_size("gx")
    flag = lambda b: jnp.where(b, 1.0, 0.0).astype(f32)
    hasn, hass, hasw, hase = flag(gy > 0), flag(gy < ny - 1), flag(gx > 0), flag(gx < nx - 1)

    meet_signal()

    def convert(k, x):
        for l in range(d.levels):
            ec[pl.ds((k * d.levels + l) * es, d.rows), :] = ens[k, l].astype(f32)
        return x

    lax.fori_loop(0, d.members, convert, 0)

    def transpose_row(r):
        parts = []
        for h in range(d.halves):
            for f in range(0, d.fields, 8):
                parts.append(ec[pl.ds(f * es + h * d.r + r, 8, stride=es), :])
        et[pl.ds(BASE + (r + D) * d.st + D, d.cols), :] = jnp.concatenate(parts, axis=0).T

    for r in list(range(4)) + list(range(d.r - 4, d.r)):
        transpose_row(r)
    ens_send_rows(d, et, hn, hs)
    meet_wait()
    ecopies = [send(N_, hn, ls, esem, rsem), send(S_, hs, ln, esem, rsem)]

    def more(q, x):
        for s in range(4):
            transpose_row(q * 4 + s)
        return x

    lax.fori_loop(1, d.r // 4 - 1, more, 0)
    for r in range(d.r):
        at = BASE + (r + D) * d.st + D
        hw[r * 4:r * 4 + 4, :] = et[at:at + 4, :]
        he[r * 4:r * 4 + 4, :] = et[at + d.cols - 4:at + d.cols, :]
    n4 = d.r * 4
    ecopies += [send(W_, hw, le, esem, rsem), send(E_, he, lw, esem, rsem),
                send(NW, hw.at[0:16], lse, esem, rsem), send(NE, he.at[0:16], lsw, esem, rsem),
                send(SW, hw.at[n4 - 16:n4], lne, esem, rsem), send(SE, he.at[n4 - 16:n4], lnw, esem, rsem)]

    scatter(d, cell, level, inn, wt, go, do)
    gr[...] = jnp.zeros_like(gr)
    dr[...] = jnp.zeros_like(dr)
    gcopies = exchange(d, [(go, gr), (do, dr)], ex0)
    build_selectors(d, sel, bsel)
    p = lax.broadcasted_iota(jnp.int32, (d.groups * 8, LANES), 0)
    cm[...] = jnp.where(p < D, hasw, jnp.where(p >= D + d.cols, hase, 1.0))
    low8 = lane_iota(8) < LANES // 2
    rt[...] = jnp.where(low8, hasn, 1.0)
    rb[...] = jnp.where(low8, 1.0, hass)

    zero = lambda n: jnp.zeros((n, LANES), f32)
    for ref, ext in ((pad, 0), (b1, 1), (b2, 2), (b3, 3)):
        for r in range(-min(ext + 2, D), d.r + min(ext + 2, D)):
            at = BASE + (r + D) * d.st
            if r < -ext or r >= d.r + ext:
                ref[at:at + d.st, :] = zero(d.st)
            else:
                ref[at + d.groups * 8:at + d.st, :] = zero(d.st - d.groups * 8)
                if ext == 0:
                    ref[at:at + D, :] = zero(D)
                    ref[at + D + d.cols:at + d.groups * 8, :] = zero(D)
        ref[0:BASE, :] = zero(BASE)
        ref[BASE + d.rr * d.st:d.size, :] = zero(8)

    for c in ecopies:
        c.wait_recv()
    low = lane_iota(d.cols) < LANES // 2
    row_at = lambda r: BASE + (r + D) * d.st
    own = lambda r: et[row_at(r) + D:row_at(r) + D + d.cols, :]
    for j in range(D):
        south = ls[j % 2] * hass
        north = ln[j % 2] * hasn
        if j < 2:
            sv = flip(jnp.where(low, south, own(j)))
            nv = flip(jnp.where(low, own(d.r - 4 + j), north))
        else:
            sv = jnp.where(low, flip(own(j)), south)
            nv = jnp.where(low, north, flip(own(d.r - 4 + j)))
        et[row_at(d.r + j) + D:row_at(d.r + j) + D + d.cols, :] = sv
        et[row_at(j - D) + D:row_at(j - D) + D + d.cols, :] = nv
    low16 = lane_iota(16) < LANES // 2
    for land, north, south, ok, off in ((lw, lnw, lsw, hasw, 0), (le, lne, lse, hase, D + d.cols)):
        for r in range(d.r):
            et[row_at(r) + off:row_at(r) + off + 4, :] = land[r * 4:r * 4 + 4, :] * ok
        nv = flip(jnp.where(low16, land[n4 - 16:n4, :], north[...] * hasn)) * ok
        sv = flip(jnp.where(low16, south[...] * hass, land[0:16, :])) * ok
        for j in range(D):
            et[row_at(j - D) + off:row_at(j - D) + off + 4, :] = nv[j * 4:j * 4 + 4, :]
            et[row_at(d.r + j) + off:row_at(d.r + j) + off + 4, :] = sv[j * 4:j * 4 + 4, :]

    def g_step(g_o, g_r, po, out, n, yo, yr):
        expand(d, g_o, g_r, sel, et, u)
        half_filter(d, u, (a1, a2, a3), pad, po, masks)
        copy = pltpu.make_async_copy(po, out, osem.at[n])
        copy.start()
        back_filter(d, pad, (b1, b2, b3), et, lhs, masks)
        reduce_members(d, lhs, bsel, yo, yr)
        return copy

    o0 = g_step(go, gr, po0, p0_out, 0, y0o, y0r)
    ycopies = exchange(d, [(y0o, y0r)], ex1)
    g1o[...] = do[...] * y0o[...]
    g1r[...] = dr[...] * y0r[...]
    o1 = g_step(g1o, g1r, po1, p1_out, 1, y1o, y1r)
    zcopies = exchange(d, [(y1o, y1r)], ex2)
    inner = slice(D, D + d.cols)
    y0, y1, g0, g1, dd = y0o[inner, :], y1o[inner, :], go[inner, :], g1o[inner, :], do[inner, :]
    x_ref[...] = jnp.zeros_like(x_ref)
    for k, v in enumerate((g0 * y0, g1 * y0, g1 * y1, dd * y1 * y1)):
        x_ref[k:k + 1, :] = jnp.sum(v, axis=0, keepdims=True)
    y0_out[...] = y0
    y1_out[...] = y1
    all_sum(x_ref, m_out, mid_ref, ra_ref, rb_ref, sa, qa, sb, qb)
    for c in ecopies + gcopies + ycopies + zcopies:
        c.wait_send()
    o0.wait()
    o1.wait()


def final_kernel(d, p0, p1, y0, y1, m_ref, c_ref, inc_ref):
    m = jnp.sum(m_ref[...], axis=1, keepdims=True)
    m = [m[k:k + 1] for k in range(4)]
    bn2 = m[0] + EPS
    c = (EPS - m[1]) / bn2
    alpha1 = (m[0] + m[1]) / bn2
    r2 = jnp.maximum((c * c * m[0] + 2.0 * c * m[1] + m[2]) / bn2, 0.0)
    rho = (c * c * m[1] + 2.0 * c * m[2] + m[3]) / bn2
    b2 = r2 + EPS
    alpha2 = (r2 + rho) / b2
    det = alpha1 * alpha2 - b2
    ca, cb = (alpha2 - c) / det, -1.0 / det
    wide = lambda v: jnp.broadcast_to(v, (LANES, LANES))
    scale = KAPPA ** SWEEPS
    sa, sb = wide(ca * scale), wide(cb * scale)
    inc = (wide(ca) * y0[...] + wide(cb) * y1[...]).T
    for l in range(d.levels):
        inc_ref[l] = inc[l * d.rows:(l + 1) * d.rows]
    step = p0.shape[0]
    for r in range(step):
        v = (sa * p0[r] + sb * p1[r]).T
        for h in range(d.halves):
            for f in range(0, d.fields, 8):
                at = h * d.fields + f
                c_ref[pl.ds((f * d.halves + h) * step + r, 8, stride=d.halves * step), :] = v[at:at + 8]


def on_device(ensemble, obs_cell, obs_level, innovation, obs_weight):
    members, levels, rows, cols = ensemble.shape
    d = Dims(members, levels, rows, cols)
    nx, ny = lax.axis_size("gx"), lax.axis_size("gy")
    vm = pl.BlockSpec(memory_space=pltpu.VMEM)
    hbm = pl.BlockSpec(memory_space=pltpu.HBM)
    dma = pltpu.SemaphoreType.DMA
    v = lambda *s: pltpu.VMEM(s, f32)
    flat = lambda a: a.reshape(1, -1)
    shape = lambda *s: jax.ShapeDtypeStruct(s, f32)
    scratch = [v(d.fields * (rows + 1), LANES)] + [v(d.size, LANES)] * 9
    scratch += [pltpu.VMEM((d.rr // 2, 256, 256), bf16), pltpu.VMEM((d.rr * 256, LANES), bf16),
                pltpu.VMEM((d.st, d.rr * 256), bf16), v(d.r, cols, LANES), v(d.r, cols, LANES)]
    scratch += [v(d.groups * 8, LANES), v(8, LANES), v(8, LANES)]
    side = d.r * 4
    scratch += [v(2, cols, LANES), v(2, cols, LANES), v(side, LANES), v(side, LANES)] * 2
    scratch += [v(16, LANES)] * 4 + [dma((8,)), dma((8,))]
    scratch += [v(d.st, LANES)] * 10
    scratch += exchange_buffers(2) + exchange_buffers(1) + exchange_buffers(1)
    scratch += [v(8, LANES), v(8, LANES), v(nx - 1, 8, LANES), v(ny - 1, 8, LANES), dma((nx - 1,)), dma((nx - 1,)),
                dma((ny - 1,)), dma((ny - 1,)), dma((2,))]

    def main_entry(*refs):
        main_kernel(d, *refs)

    def final_entry(*refs):
        final_kernel(d, *refs)

    p0, p1, y0, y1, m = pl.pallas_call(
        main_entry,
        out_shape=(shape(d.r, cols, LANES), shape(d.r, cols, LANES), shape(cols, LANES), shape(cols, LANES), shape(8, LANES)),
        in_specs=[vm] * 5,
        out_specs=(hbm, hbm, vm, vm, vm),
        scratch_shapes=scratch,
        compiler_params=pltpu.CompilerParams(collective_id=0, has_side_effects=True, vmem_limit_bytes=64000000),
    )(ensemble, flat(obs_cell), flat(obs_level), flat(innovation), flat(obs_weight))
    step = 8
    block = d.fields * d.halves * step
    full = lambda *s: pl.BlockSpec(s, lambda i: (0,) * len(s))
    out4 = (d.r // step, block, LANES)

    def final_grid(p0, p1, y0, y1, m, c_ref, inc_ref, buf, sem):
        i = pl.program_id(0)
        steps = pl.num_programs(0)
        slot = lax.rem(i, 2)

        def copy(j, k):
            return pltpu.make_async_copy(
                buf.at[k].reshape(d.fields * d.halves, step, LANES),
                c_ref.at[:, pl.ds(pl.multiple_of(j * step, step), step), :], sem.at[k])

        @pl.when(i >= 2)
        def _():
            copy(i - 2, slot).wait()

        final_kernel(d, p0, p1, y0, y1, m, buf.at[slot], inc_ref)
        copy(i, slot).start()

        @pl.when(i == steps - 1)
        def _():
            copy(i - 1, 1 - slot).wait()
            copy(i, slot).wait()

    control, increment = pl.pallas_call(
        final_grid,
        grid=(d.r // step,),
        out_shape=(shape(d.fields * d.halves, d.r, LANES), shape(levels, rows, cols)),
        in_specs=[pl.BlockSpec((step, cols, LANES), lambda i: (i, 0, 0))] * 2 + [full(cols, LANES)] * 2 + [full(8, LANES)],
        out_specs=(hbm, full(levels, rows, cols)),
        scratch_shapes=[v(2, block, LANES), dma((2,))],
        compiler_params=pltpu.CompilerParams(vmem_limit_bytes=20000000),
    )(p0, p1, y0, y1, m)
    return (control.reshape(members, levels, rows, cols), increment)


def solution(mesh):
    return jax.shard_map(
        on_device,
        mesh=mesh,
        in_specs=(
            P(None, None, "gy", "gx"),
            P("gy", "gx", None),
            P("gy", "gx", None),
            P("gy", "gx", None),
            P("gy", "gx", None),
        ),
        out_specs=(P(None, None, "gy", "gx"), P(None, "gy", "gx")),
        check_vma=False,
    )
```

time: 81.2 us -> 58.2 us (0.72)
  Pallas kernels: 76.6 us -> 51.7 us
  local copies, waits for them, and re-layouts: 3.82 us -> 5.52 us
    pallas_call x1 -> x2, Pallas kernels: 76.6 us -> 51.7 us  [the longest x1 48.2 us: on_device(): pl.pallas_call(main_entry, out_shape=(shape(d.r, cols, LANES), shape(d.r,...]
    unnamed x4 -> x10, local copies, waits for them, and re-layouts: 3.82 us -> 5.52 us
where the time goes in v1:
time: 58.2 us; the launch traced here: 57.9 us
  Pallas kernels  51.7 us (89%)
  local copies, waits for them, and re-layouts  5.52 us (9%)
  between operations  0.65 us (1%)
    pallas_call x1, Pallas kernels, on_device(): pl.pallas_call(main_entry, out_shape=(shape(d.r, cols, LANES), shape(d.r,...  48.2 us
    unnamed x10, local copies, waits for them, and re-layouts  5.52 us
    pallas_call x1, Pallas kernels, on_device(): pl.pallas_call(final_grid, grid=(d.r // step,), out_shape=(shape(d.fields...  3.51 us

profile of v1, /device:TPU:0, one launch (start us, length us, event | category | flops | bytes accessed | tf_op | source)
XLA Modules:
  0.0 57.9 jit_solution(1926904648806579261)
XLA Ops:
  0.6 48.2 %shard_map.68 = (f32[32,128,128]{2,1,0:T(8,128)}, f32[32,128,128]{2,1,0:T(8,128)}, f32[128,128]{1,0:T(8,128)}, f32[128,128]{1,0:T(8,128)}, f32[8,128]{1,0:T(8,128)}) custom-call(bf16[32,2,64,128]{3,2,1,0:T(8,128)(2,1)} %refs_0_.1, s32[1,2048]{1,0:T(1,128)} %bitcast.5, s32[1,2048]{1,0:T(1,128)} %bitcast.6, f32[1,2048]{1,0:T(1,128)} %bitcast.7, f32[1,2048]{1,0:T(1,128)} %bitcast.8), custom_call_target="tpu_custom_call" | custom-call | tf_op jit(solution)/shard_map/pallas_call | solution.py:520
  48.9 0.0 copy-start
  48.9 1.6 %copy-done = f32[32,128,128]{2,1,0:T(8,128)S(1)} copy-done((f32[32,128,128]{2,1,0:T(8,128)S(1)}, f32[32,128,128]{2,1,0:T(8,128)}, u32[]{:S(2)}) %copy-start) | copy-done | bytes 2097176
  50.4 0.0 copy-start.1
  50.4 1.6 %copy-done.1 = f32[32,128,128]{2,1,0:T(8,128)S(1)} copy-done((f32[32,128,128]{2,1,0:T(8,128)S(1)}, f32[32,128,128]{2,1,0:T(8,128)}, u32[]{:S(2)}) %copy-start.1) | copy-done | bytes 2097176
  52.0 0.0 copy-start.2
  52.0 0.8 %copy-done.2 = f32[128,128]{1,0:T(8,128)S(1)} copy-done((f32[128,128]{1,0:T(8,128)S(1)}, f32[128,128]{1,0:T(8,128)}, u32[]{:S(2)}) %copy-start.2) | copy-done | bytes 65560
  52.9 0.0 copy-start.3
  52.9 0.8 %copy-done.3 = f32[128,128]{1,0:T(8,128)S(1)} copy-done((f32[128,128]{1,0:T(8,128)S(1)}, f32[128,128]{1,0:T(8,128)}, u32[]{:S(2)}) %copy-start.3) | copy-done | bytes 65560
  53.7 0.0 copy-start.4
  53.7 0.7 %copy-done.4 = f32[8,128]{1,0:T(8,128)S(1)} copy-done((f32[8,128]{1,0:T(8,128)S(1)}, f32[8,128]{1,0:T(8,128)}, u32[]{:S(2)}) %copy-start.4) | copy-done | bytes 4120
  54.4 3.5 %shard_map.69 = (f32[128,32,128]{2,1,0:T(8,128)}, f32[2,64,128]{2,1,0:T(8,128)}) custom-call(f32[32,128,128]{2,1,0:T(8,128)S(1)} %copy-done, f32[32,128,128]{2,1,0:T(8,128)S(1)} %copy-done.1, f32[128,128]{1,0:T(8,128)S(1)} %copy-done.2, f32[128,128]{1,0:T(8,128)S(1)} %copy-done.3, f32[8,128]{1,0:T(8,128)S(1)} %copy-done.4), custom_call_target="tpu_custom_call" | custom-call | tf_op jit(solution)/shard_map/pallas_call | solution.py:555
Async XLA Ops:
  48.9 1.6 %copy-start = (f32[32,128,128]{2,1,0:T(8,128)S(1)}, f32[32,128,128]{2,1,0:T(8,128)}, u32[]{:S(2)}) copy-start(f32[32,128,128]{2,1,0:T(8,128)} %get-tuple-element.9.p0) | copy-start | bytes 6291460
  50.4 1.6 %copy-start.1 = (f32[32,128,128]{2,1,0:T(8,128)S(1)}, f32[32,128,128]{2,1,0:T(8,128)}, u32[]{:S(2)}) copy-start(f32[32,128,128]{2,1,0:T(8,128)} %get-tuple-element.10.p1) | copy-start | bytes 6291460
  52.0 0.8 %copy-start.2 = (f32[128,128]{1,0:T(8,128)S(1)}, f32[128,128]{1,0:T(8,128)}, u32[]{:S(2)}) copy-start(f32[128,128]{1,0:T(8,128)} %get-tuple-element.11.y0) | copy-start | bytes 196612
  52.9 0.8 %copy-start.3 = (f32[128,128]{1,0:T(8,128)S(1)}, f32[128,128]{1,0:T(8,128)}, u32[]{:S(2)}) copy-start(f32[128,128]{1,0:T(8,128)} %get-tuple-element.12.y1) | copy-start | bytes 196612
  53.7 0.7 %copy-start.4 = (f32[8,128]{1,0:T(8,128)S(1)}, f32[8,128]{1,0:T(8,128)}, u32[]{:S(2)}) copy-start(f32[8,128]{1,0:T(8,128)} %get-tuple-element.13.m) | copy-start | bytes 12292

commit v2 on v1

--- a/solution.py
+++ b/solution.py
@@ -37,27 +37,52 @@
     return {"gy": lax.rem(lax.axis_index("gy") + dy + ny, ny), "gx": lax.rem(lax.axis_index("gx") + dx + nx, nx)}
 
 
+def others():
+    ny, nx = lax.axis_size("gy"), lax.axis_size("gx")
+    return [(dy, dx) for dy in range(ny) for dx in range(nx) if dy or dx]
+
+
 def meet_signal():
     bar = pltpu.get_barrier_semaphore()
-    for dy, dx in SIDES:
+    for dy, dx in others():
         pl.semaphore_signal(bar, inc=1, device_id=peer(dy, dx), device_id_type=MESH)
-    for axis in ("gx", "gy"):
-        n, me = lax.axis_size(axis), lax.axis_index(axis)
-        for k in range(1, n):
-            pl.semaphore_signal(bar, inc=1, device_id={axis: lax.rem(me + k, n)}, device_id_type=MESH)
 
 
 def meet_wait():
-    total = len(SIDES) + lax.axis_size("gx") + lax.axis_size("gy") - 2
-    pl.semaphore_wait(pltpu.get_barrier_semaphore(), total)
-
-
-def send(n, src, dst, ssem, rsem):
+    pl.semaphore_wait(pltpu.get_barrier_semaphore(), len(others()))
+
+
+def present(n):
     dy, dx = SIDES[n]
-    c = pltpu.make_async_remote_copy(src_ref=src, dst_ref=dst, send_sem=ssem.at[n], recv_sem=rsem.at[n],
-                                     device_id=peer(dy, dx), device_id_type=MESH)
-    c.start()
-    return c
+    gy, gx = lax.axis_index("gy") + dy, lax.axis_index("gx") + dx
+    ok = None
+    for d, i, axis in ((dy, gy, "gy"), (dx, gx, "gx")):
+        if d:
+            t = (i >= 0) if d < 0 else (i < lax.axis_size(axis))
+            ok = t if ok is None else ok & t
+    return ok
+
+
+class Side:
+    def __init__(self, n, src, dst, ssem, rsem):
+        dy, dx = SIDES[n]
+        self.n = n
+        self.copy = pltpu.make_async_remote_copy(src_ref=src, dst_ref=dst, send_sem=ssem.at[n], recv_sem=rsem.at[n],
+                                                 device_id=peer(dy, dx), device_id_type=MESH)
+        pl.when(present(n))(self.copy.start)
+
+    def wait_recv(self):
+        pl.when(present(BACK[self.n]))(self.copy.wait_recv)
+
+    def wait_send(self):
+        pl.when(present(self.n))(self.copy.wait_send)
+
+
+def clear_absent(n, refs):
+    @pl.when(jnp.logical_not(present(n)))
+    def _():
+        for ref in refs:
+            ref[...] = jnp.zeros_like(ref)
 
 
 def lane_iota(rows):
@@ -126,7 +151,7 @@
         for k in range(2):
             for j in range(3):
                 out[k][a, j] = packs[k][j]
-    copies = [send(n, out[n], land[BACK[n]], ssem, rsem) for n in (N_, S_, W_, E_, NW, NE, SW, SE)]
+    copies = [Side(n, out[n], land[BACK[n]], ssem, rsem) for n in (N_, S_, W_, E_, NW, NE, SW, SE)]
     for c in copies:
         c.wait_recv()
     for a, (yo, yr) in enumerate(pairs):
@@ -293,30 +318,19 @@
     yr[...] = (dot(0, k0) + dot(k1, k2)) * scale
 
 
-def all_sum(x_ref, o_ref, mid_ref, ra_ref, rb_ref, sa, qa, sb, qb):
-    nx, ny = lax.axis_size("gx"), lax.axis_size("gy")
-    mx, my = lax.axis_index("gx"), lax.axis_index("gy")
-
-    def stage(axis, n, me, src, land, ssem, rsem):
-        copies = []
-        for k in range(1, n):
-            copies.append(pltpu.make_async_remote_copy(
-                src_ref=src, dst_ref=land.at[k - 1], send_sem=ssem.at[k - 1], recv_sem=rsem.at[k - 1],
-                device_id={axis: lax.rem(me + k, n)}, device_id_type=MESH))
-            copies[-1].start()
-        for c in copies:
-            c.wait_recv()
-        total = src[...]
-        for k in range(n - 1):
-            total = total + land[k]
-        return copies, total
-
-    ca, total = stage("gx", nx, mx, x_ref, ra_ref, sa, qa)
-    mid_ref[...] = total
-    cb, total = stage("gy", ny, my, mid_ref, rb_ref, sb, qb)
-    o_ref[...] = total
-    for c in ca + cb:
-        c.wait_send()
+def all_sum(x_ref, land, ssem, rsem):
+    copies = []
+    for k, (dy, dx) in enumerate(others()):
+        copies.append(pltpu.make_async_remote_copy(
+            src_ref=x_ref, dst_ref=land.at[k], send_sem=ssem.at[k], recv_sem=rsem.at[k],
+            device_id=peer(dy, dx), device_id_type=MESH))
+        copies[-1].start()
+    for c in copies:
+        c.wait_recv()
+    total = x_ref[...]
+    for k in range(len(copies)):
+        total = total + land[k]
+    return copies, total
 
 
 def ens_send_rows(d, et, hn, hs):
@@ -328,7 +342,7 @@
         hs[i] = jnp.where(low, flip(at(d.r - 2 + i)), at(d.r - 4 + i))
 
 
-def main_kernel(d, ens, cell, level, inn, wt, p0_out, p1_out, y0_out, y1_out, m_out, *refs):
+def main_kernel(d, ens_in, cell_in, level_in, inn_in, wt_in, p0_out, p1_out, ym_out, *refs):
     refs = list(refs)
     take = lambda n: [refs.pop(0) for _ in range(n)]
     ec, et, u, a1, a2, a3, pad, b1, b2, b3 = take(10)
@@ -337,8 +351,8 @@
     hn, hs, hw, he, ln, ls, lw, le, lnw, lne, lsw, lse, esem, rsem = take(14)
     go, gr, do, dr, g1o, g1r, y0o, y0r, y1o, y1r = take(10)
     ex0, ex1, ex2 = take(18), take(18), take(18)
-    x_ref, mid_ref, ra_ref, rb_ref, sa, qa, sb, qb = take(8)
-    osem = refs.pop(0)
+    x_ref, sum_land, sum_s, sum_r = take(4)
+    ens, cell, level, inn, wt, isem, osem = take(7)
     es = d.rows + 1
     gy, gx = lax.axis_index("gy"), lax.axis_index("gx")
     ny, nx = lax.axis_size("gy"), lax.axis_size("gx")
@@ -346,13 +360,24 @@
     hasn, hass, hasw, hase = flag(gy > 0), flag(gy < ny - 1), flag(gx > 0), flag(gx < nx - 1)
 
     meet_signal()
+    chunk = d.members // 4
+    loads = [pltpu.make_async_copy(ens_in.at[pl.ds(k * chunk, chunk)], ens.at[pl.ds(k * chunk, chunk)], isem.at[k])
+             for k in range(4)]
+    small = [pltpu.make_async_copy(a, b, isem.at[4 + k])
+             for k, (a, b) in enumerate(((cell_in, cell), (level_in, level), (inn_in, inn), (wt_in, wt)))]
+    for c in loads + small:
+        c.start()
+    for n, refs_n in enumerate(((ln,), (ls,), (lw,), (le,), (lnw,), (lne,), (lsw,), (lse,))):
+        clear_absent(n, refs_n + tuple(ex[8 + n] for ex in (ex0, ex1, ex2)))
 
     def convert(k, x):
         for l in range(d.levels):
             ec[pl.ds((k * d.levels + l) * es, d.rows), :] = ens[k, l].astype(f32)
         return x
 
-    lax.fori_loop(0, d.members, convert, 0)
+    for k in range(4):
+        loads[k].wait()
+        lax.fori_loop(k * chunk, (k + 1) * chunk, convert, 0)
 
     def transpose_row(r):
         parts = []
@@ -361,26 +386,26 @@
                 parts.append(ec[pl.ds(f * es + h * d.r + r, 8, stride=es), :])
         et[pl.ds(BASE + (r + D) * d.st + D, d.cols), :] = jnp.concatenate(parts, axis=0).T
 
-    for r in list(range(4)) + list(range(d.r - 4, d.r)):
-        transpose_row(r)
+    def transpose_four(q):
+        for t in range(4):
+            transpose_row(q * 4 + t)
+        for t in range(4):
+            r = q * 4 + t
+            at = BASE + (r + D) * d.st + D
+            to = pl.ds(pl.multiple_of(r * 4, 4), 4)
+            hw[to, :] = et[pl.ds(at, 4), :]
+            he[to, :] = et[pl.ds(at + d.cols - 4, 4), :]
+
+    lax.fori_loop(0, d.r // 4, lambda q, x: (transpose_four(q), x)[1], 0)
     ens_send_rows(d, et, hn, hs)
+    n4 = d.r * 4
     meet_wait()
-    ecopies = [send(N_, hn, ls, esem, rsem), send(S_, hs, ln, esem, rsem)]
-
-    def more(q, x):
-        for s in range(4):
-            transpose_row(q * 4 + s)
-        return x
-
-    lax.fori_loop(1, d.r // 4 - 1, more, 0)
-    for r in range(d.r):
-        at = BASE + (r + D) * d.st + D
-        hw[r * 4:r * 4 + 4, :] = et[at:at + 4, :]
-        he[r * 4:r * 4 + 4, :] = et[at + d.cols - 4:at + d.cols, :]
-    n4 = d.r * 4
-    ecopies += [send(W_, hw, le, esem, rsem), send(E_, he, lw, esem, rsem),
-                send(NW, hw.at[0:16], lse, esem, rsem), send(NE, he.at[0:16], lsw, esem, rsem),
-                send(SW, hw.at[n4 - 16:n4], lne, esem, rsem), send(SE, he.at[n4 - 16:n4], lnw, esem, rsem)]
+    ecopies = [Side(N_, hn, ls, esem, rsem), Side(S_, hs, ln, esem, rsem),
+               Side(W_, hw, le, esem, rsem), Side(E_, he, lw, esem, rsem),
+               Side(NW, hw.at[0:16], lse, esem, rsem), Side(NE, he.at[0:16], lsw, esem, rsem),
+               Side(SW, hw.at[n4 - 16:n4], lne, esem, rsem), Side(SE, he.at[n4 - 16:n4], lnw, esem, rsem)]
+    for c in small:
+        c.wait()
 
     scatter(d, cell, level, inn, wt, go, do)
     gr[...] = jnp.zeros_like(gr)
@@ -413,8 +438,8 @@
     row_at = lambda r: BASE + (r + D) * d.st
     own = lambda r: et[row_at(r) + D:row_at(r) + D + d.cols, :]
     for j in range(D):
-        south = ls[j % 2] * hass
-        north = ln[j % 2] * hasn
+        south = ls[j % 2]
+        north = ln[j % 2]
         if j < 2:
             sv = flip(jnp.where(low, south, own(j)))
             nv = flip(jnp.where(low, own(d.r - 4 + j), north))
@@ -424,11 +449,11 @@
         et[row_at(d.r + j) + D:row_at(d.r + j) + D + d.cols, :] = sv
         et[row_at(j - D) + D:row_at(j - D) + D + d.cols, :] = nv
     low16 = lane_iota(16) < LANES // 2
-    for land, north, south, ok, off in ((lw, lnw, lsw, hasw, 0), (le, lne, lse, hase, D + d.cols)):
+    for land, north, south, off in ((lw, lnw, lsw, 0), (le, lne, lse, D + d.cols)):
         for r in range(d.r):
-            et[row_at(r) + off:row_at(r) + off + 4, :] = land[r * 4:r * 4 + 4, :] * ok
-        nv = flip(jnp.where(low16, land[n4 - 16:n4, :], north[...] * hasn)) * ok
-        sv = flip(jnp.where(low16, south[...] * hass, land[0:16, :])) * ok
+            et[row_at(r) + off:row_at(r) + off + 4, :] = land[r * 4:r * 4 + 4, :]
+        nv = flip(jnp.where(low16, land[n4 - 16:n4, :], north[...]))
+        sv = flip(jnp.where(low16, south[...], land[0:16, :]))
         for j in range(D):
             et[row_at(j - D) + off:row_at(j - D) + off + 4, :] = nv[j * 4:j * 4 + 4, :]
             et[row_at(d.r + j) + off:row_at(d.r + j) + off + 4, :] = sv[j * 4:j * 4 + 4, :]
@@ -450,21 +475,25 @@
     zcopies = exchange(d, [(y1o, y1r)], ex2)
     inner = slice(D, D + d.cols)
     y0, y1, g0, g1, dd = y0o[inner, :], y1o[inner, :], go[inner, :], g1o[inner, :], do[inner, :]
-    x_ref[...] = jnp.zeros_like(x_ref)
+    lane1 = lane_iota(1)
+    x = jnp.zeros((1, LANES), f32)
     for k, v in enumerate((g0 * y0, g1 * y0, g1 * y1, dd * y1 * y1)):
-        x_ref[k:k + 1, :] = jnp.sum(v, axis=0, keepdims=True)
-    y0_out[...] = y0
-    y1_out[...] = y1
-    all_sum(x_ref, m_out, mid_ref, ra_ref, rb_ref, sa, qa, sb, qb)
-    for c in ecopies + gcopies + ycopies + zcopies:
+        t = jnp.sum(jnp.sum(v, axis=0, keepdims=True), axis=1, keepdims=True)
+        x = jnp.where(lane1 == k, t, x)
+    x_ref[...] = x
+    ym_out[0:d.cols, :] = y0
+    ym_out[d.cols:2 * d.cols, :] = y1
+    scopies, total = all_sum(x_ref, sum_land, sum_s, sum_r)
+    ym_out[2 * d.cols:2 * d.cols + 8, :] = jnp.broadcast_to(total, (8, LANES))
+    for c in ecopies + gcopies + ycopies + zcopies + scopies:
         c.wait_send()
     o0.wait()
     o1.wait()
 
 
-def final_kernel(d, p0, p1, y0, y1, m_ref, c_ref, inc_ref):
-    m = jnp.sum(m_ref[...], axis=1, keepdims=True)
-    m = [m[k:k + 1] for k in range(4)]
+def final_kernel(d, p0, p1, ym, c_ref, inc_ref):
+    y0, y1, m = ym[0:d.cols], ym[d.cols:2 * d.cols], ym[2 * d.cols:2 * d.cols + 1]
+    m = [m[:, k:k + 1] for k in range(4)]
     bn2 = m[0] + EPS
     c = (EPS - m[1]) / bn2
     alpha1 = (m[0] + m[1]) / bn2
@@ -477,7 +506,7 @@
     wide = lambda v: jnp.broadcast_to(v, (LANES, LANES))
     scale = KAPPA ** SWEEPS
     sa, sb = wide(ca * scale), wide(cb * scale)
-    inc = (wide(ca) * y0[...] + wide(cb) * y1[...]).T
+    inc = (wide(ca) * y0 + wide(cb) * y1).T
     for l in range(d.levels):
         inc_ref[l] = inc[l * d.rows:(l + 1) * d.rows]
     step = p0.shape[0]
@@ -508,20 +537,20 @@
     scratch += [v(16, LANES)] * 4 + [dma((8,)), dma((8,))]
     scratch += [v(d.st, LANES)] * 10
     scratch += exchange_buffers(2) + exchange_buffers(1) + exchange_buffers(1)
-    scratch += [v(8, LANES), v(8, LANES), v(nx - 1, 8, LANES), v(ny - 1, 8, LANES), dma((nx - 1,)), dma((nx - 1,)),
-                dma((ny - 1,)), dma((ny - 1,)), dma((2,))]
+    n = nx * ny - 1
+    obs = obs_cell.shape[-1]
+    scratch += [v(1, LANES), v(n, 1, LANES), dma((n,)), dma((n,))]
+    scratch += [pltpu.VMEM(ensemble.shape, bf16)] + [pltpu.VMEM((1, obs), jnp.int32)] * 2 + [v(1, obs)] * 2
+    scratch += [dma((8,)), dma((2,))]
 
     def main_entry(*refs):
         main_kernel(d, *refs)
 
-    def final_entry(*refs):
-        final_kernel(d, *refs)
-
-    p0, p1, y0, y1, m = pl.pallas_call(
+    p0, p1, ym = pl.pallas_call(
         main_entry,
-        out_shape=(shape(d.r, cols, LANES), shape(d.r, cols, LANES), shape(cols, LANES), shape(cols, LANES), shape(8, LANES)),
-        in_specs=[vm] * 5,
-        out_specs=(hbm, hbm, vm, vm, vm),
+        out_shape=(shape(d.r, cols, LANES), shape(d.r, cols, LANES), shape(2 * cols + 8, LANES)),
+        in_specs=[hbm] * 5,
+        out_specs=(hbm, hbm, vm),
         scratch_shapes=scratch,
         compiler_params=pltpu.CompilerParams(collective_id=0, has_side_effects=True, vmem_limit_bytes=64000000),
     )(ensemble, flat(obs_cell), flat(obs_level), flat(innovation), flat(obs_weight))
@@ -530,7 +559,7 @@
     full = lambda *s: pl.BlockSpec(s, lambda i: (0,) * len(s))
     out4 = (d.r // step, block, LANES)
 
-    def final_grid(p0, p1, y0, y1, m, c_ref, inc_ref, buf, sem):
+    def final_grid(p0, p1, ym, c_ref, inc_ref, buf, sem):
         i = pl.program_id(0)
         steps = pl.num_programs(0)
         slot = lax.rem(i, 2)
@@ -544,7 +573,7 @@
         def _():
             copy(i - 2, slot).wait()
 
-        final_kernel(d, p0, p1, y0, y1, m, buf.at[slot], inc_ref)
+        final_kernel(d, p0, p1, ym, buf.at[slot], inc_ref)
         copy(i, slot).start()
 
         @pl.when(i == steps - 1)
@@ -556,11 +585,11 @@
         final_grid,
         grid=(d.r // step,),
         out_shape=(shape(d.fields * d.halves, d.r, LANES), shape(levels, rows, cols)),
-        in_specs=[pl.BlockSpec((step, cols, LANES), lambda i: (i, 0, 0))] * 2 + [full(cols, LANES)] * 2 + [full(8, LANES)],
+        in_specs=[pl.BlockSpec((step, cols, LANES), lambda i: (i, 0, 0))] * 2 + [full(2 * cols + 8, LANES)],
         out_specs=(hbm, full(levels, rows, cols)),
         scratch_shapes=[v(2, block, LANES), dma((2,))],
-        compiler_params=pltpu.CompilerParams(vmem_limit_bytes=20000000),
-    )(p0, p1, y0, y1, m)
+        compiler_params=pltpu.CompilerParams(vmem_limit_bytes=64000000),
+    )(p0, p1, ym)
     return (control.reshape(members, levels, rows, cols), increment)
 
 

time: 58.2 us -> 50.5 us (0.87)
  local copies, waits for them, and re-layouts: 5.52 us -> 0 us
  Pallas kernels: 51.7 us -> 49.7 us
    unnamed x10 -> x0, local copies, waits for them, and re-layouts: 5.52 us -> none
    pallas_call x1, Pallas kernels: 48.2 us -> 43.7 us  [on_device(): pl.pallas_call(main_entry, out_shape=(shape(d.r, cols, LANES), shape(d.r,...]
    pallas_call x1, Pallas kernels: 3.51 us -> 6.01 us  [on_device(): pl.pallas_call(final_grid, grid=(d.r // step,), out_shape=(shape(d.fields...]
where the time goes in v2:
time: 50.5 us; the launch traced here: 50.3 us
  Pallas kernels  49.7 us (98%)
  between operations  0.64 us (1%)
    pallas_call x1, Pallas kernels, on_device(): pl.pallas_call(main_entry, out_shape=(shape(d.r, cols, LANES), shape(d.r,...  43.7 us
    pallas_call x1, Pallas kernels, on_device(): pl.pallas_call(final_grid, grid=(d.r // step,), out_shape=(shape(d.fields...  6.01 us

profile of v2, /device:TPU:0, one launch (start us, length us, event | category | flops | bytes accessed | tf_op | source)
XLA Modules:
  0.0 50.3 jit_solution(12312814201789181541)
XLA Ops:
  0.6 43.7 %shard_map.68 = (f32[32,128,128]{2,1,0:T(8,128)}, f32[32,128,128]{2,1,0:T(8,128)}, f32[264,128]{1,0:T(8,128)}) custom-call(bf16[32,2,64,128]{3,2,1,0:T(8,128)(2,1)} %refs_0_.1, s32[1,2048]{1,0:T(1,128)} %bitcast.5, s32[1,2048]{1,0:T(1,128)} %bitcast.6, f32[1,2048]{1,0:T(1,128)} %bitcast.7, f32[1,2048]{1,0:T(1,128)} %bitcast.8), custom_call_target="tpu_custom_call" | custom-call | tf_op jit(solution)/shard_map/pallas_call | solution.py:549
  44.3 6.0 %shard_map.69 = (f32[128,32,128]{2,1,0:T(8,128)}, f32[2,64,128]{2,1,0:T(8,128)}) custom-call(f32[32,128,128]{2,1,0:T(8,128)} %get-tuple-element.7.p0, f32[32,128,128]{2,1,0:T(8,128)} %get-tuple-element.8.p1, f32[264,128]{1,0:T(8,128)} %get-tuple-element.9.ym), custom_call_target="tpu_custom_call" | custom-call | tf_op jit(solution)/shard_map/pallas_call | solution.py:584

commit v3 on v2

--- a/solution.py
+++ b/solution.py
@@ -125,7 +125,7 @@
     return one + one + [dma((8,)), dma((8,))]
 
 
-def exchange(d, pairs, bufs):
+def exchange_start(d, pairs, bufs):
     out, land, ssem, rsem = bufs[:8], bufs[8:16], bufs[16], bufs[17]
     lo, hi, mid = row_masks(d, 8)
     last = d.groups - 1
@@ -151,7 +151,14 @@
         for k in range(2):
             for j in range(3):
                 out[k][a, j] = packs[k][j]
-    copies = [Side(n, out[n], land[BACK[n]], ssem, rsem) for n in (N_, S_, W_, E_, NW, NE, SW, SE)]
+    return [Side(n, out[n], land[BACK[n]], ssem, rsem) for n in (N_, S_, W_, E_, NW, NE, SW, SE)]
+
+
+def exchange_finish(d, pairs, bufs, copies):
+    land = bufs[8:16]
+    lo, hi, mid = row_masks(d, 8)
+    last = d.groups - 1
+    at = lambda g: slice(g * 8, g * 8 + 8)
     for c in copies:
         c.wait_recv()
     for a, (yo, yr) in enumerate(pairs):
@@ -171,7 +178,6 @@
             ring = ring + jnp.where(hi, north, jnp.where(lo, south, 0.0))
             yo[at(g), :] = own
             yr[at(g), :] = jnp.where(mid, own, ring)
-    return copies
 
 
 def build_selectors(d, sel, bsel):
@@ -204,21 +210,29 @@
     return hi, (x - hi.astype(f32)).astype(bf16)
 
 
-def expand(d, go, gr, sel, et, u):
-    def wide(ref):
-        hi, lo = split(ref[...])
-        return jnp.concatenate([hi, lo], axis=1)
-
-    own, ring = wide(go), wide(gr)
-    pairs = d.rr // 2
-    edge = D // 2
-    for q in range(pairs):
-        x = ring if q < edge or q >= pairs - edge else own
+def wide(ref):
+    hi, lo = split(ref[...])
+    return jnp.concatenate([hi, lo], axis=1)
+
+
+def expand(d, x, pairs, sel, et, u):
+    n = d.groups * 8
+    for q in pairs:
         g2 = jnp.dot(x, sel[q], preferred_element_type=f32)
         for s in range(2):
             at = BASE + (2 * q + s) * d.st
-            n = d.groups * 8
             u[at:at + n, :] = et[at:at + n, :] * g2[0:n, s * LANES:(s + 1) * LANES]
+
+
+def expand_edges(d, x, pairs, sel, et, u):
+    n = d.groups * 8
+    x = jnp.concatenate([x[0:8], x[n - 8:n]], axis=0)
+    for q in pairs:
+        g2 = jnp.dot(x, sel[q], preferred_element_type=f32)
+        for s in range(2):
+            for k in range(2):
+                at = BASE + (2 * q + s) * d.st + k * (n - 8)
+                u[at:at + 8, :] = et[at:at + 8, :] * g2[k * 8:k * 8 + 8, s * LANES:(s + 1) * LANES]
 
 
 def stencil(d, src, p, lo, hi, use):
@@ -249,23 +263,63 @@
     lax.fori_loop(0, d.groups, body, 0)
 
 
-def half_filter(d, src, bufs, pad, po, masks):
-    a1, a2, a3 = bufs
-    sweep(d, src, a1, 3, masks)
-    sweep(d, a1, a2, 2, masks)
-    sweep(d, a2, a3, 1, masks)
-
+def sweep_part(d, src, dst, ranges, groups, masks):
     def body(g, x):
-        p = g * 8 + D
+        p = pl.multiple_of(groups[0] * 8 + g * (groups[1] * 8), 8)
+        if masks is not None:
+            cm, rt, rb = masks
+            m = cm[pl.ds(p, 8), :]
+            mt, mb = m * rt[...], m * rb[...]
 
         def use(r, v):
-            pad[pl.ds(p + (BASE + (r + D) * d.st), 8), :] = v
-            po[r, pl.ds(pl.multiple_of(g * 8, 8), 8), :] = v
-
-        stencil(d, a3, p, 0, d.r, use)
+            if masks is not None:
+                v = v * (mt if r < 0 else mb if r >= d.r else m)
+            dst[pl.ds(p + (BASE + (r + D) * d.st), 8), :] = v
+
+        for lo, hi in ranges:
+            stencil(d, src, p, lo, hi, use)
         return x
 
-    lax.fori_loop(0, d.cols // 8, body, 0)
+    lax.fori_loop(0, groups[2], body, 0)
+
+
+def last_part(d, src, pad, po, ranges, groups):
+    def body(g, x):
+        c = pl.multiple_of(groups[0] * 8 + g * (groups[1] * 8), 8)
+
+        def use(r, v):
+            pad[pl.ds(c + (D + BASE + (r + D) * d.st), 8), :] = v
+            po[r, pl.ds(c, 8), :] = v
+
+        for lo, hi in ranges:
+            stencil(d, src, c + D, lo, hi, use)
+        return x
+
+    lax.fori_loop(0, groups[2], body, 0)
+
+
+def filter_inner(d, src, bufs, pad, po, margin):
+    groups = (0, 1, d.groups) if margin == 0 else (1, 1, d.groups - 2)
+    for k, dst in enumerate(bufs):
+        m = margin + k + 1
+        sweep_part(d, src, dst, [(m, d.r - m)], groups, None)
+        src = dst
+    m = margin + SWEEPS
+    last_part(d, src, pad, po, [(m, d.r - m)], (1, 1, d.cols // 8 - 2))
+
+
+def filter_outer(d, src, bufs, pad, po, margin, masks):
+    for k, dst in enumerate(bufs):
+        m, e = margin + k + 1, SWEEPS - k - 1
+        w = 2 if margin else 1
+        sweep_part(d, src, dst, [(-e, m), (d.r - m, d.r + e)], (w, 1, d.groups - 2 * w), masks)
+        for t in range(w):
+            sweep_part(d, src, dst, [(-e, d.r + e)], (t, d.groups - w, 2), masks)
+        src = dst
+    m = margin + SWEEPS
+    n = d.cols // 8
+    last_part(d, src, pad, po, [(0, m), (d.r - m, d.r)], (1, 1, n - 2))
+    last_part(d, src, pad, po, [(0, d.r)], (0, n - 1, 2))
 
 
 def back_filter(d, pad, bufs, et, lhs, masks):
@@ -346,13 +400,13 @@
     refs = list(refs)
     take = lambda n: [refs.pop(0) for _ in range(n)]
     ec, et, u, a1, a2, a3, pad, b1, b2, b3 = take(10)
-    sel, bsel, lhs, po0, po1 = take(5)
+    sel, bsel, lhs = take(3)
     cm, rt, rb = masks = take(3)
     hn, hs, hw, he, ln, ls, lw, le, lnw, lne, lsw, lse, esem, rsem = take(14)
     go, gr, do, dr, g1o, g1r, y0o, y0r, y1o, y1r = take(10)
     ex0, ex1, ex2 = take(18), take(18), take(18)
     x_ref, sum_land, sum_s, sum_r = take(4)
-    ens, cell, level, inn, wt, isem, osem = take(7)
+    ens, cell, level, inn, wt, isem = take(6)
     es = d.rows + 1
     gy, gx = lax.axis_index("gy"), lax.axis_index("gx")
     ny, nx = lax.axis_size("gy"), lax.axis_size("gx")
@@ -410,8 +464,15 @@
     scatter(d, cell, level, inn, wt, go, do)
     gr[...] = jnp.zeros_like(gr)
     dr[...] = jnp.zeros_like(dr)
-    gcopies = exchange(d, [(go, gr), (do, dr)], ex0)
+    gpairs = [(go, gr), (do, dr)]
+    gcopies = exchange_start(d, gpairs, ex0)
     build_selectors(d, sel, bsel)
+    edge = D // 2
+    pairs = d.rr // 2
+    ring_pairs = lambda n: list(range(n)) + list(range(pairs - n, pairs))
+    a_bufs = (a1, a2, a3)
+    expand(d, wide(go), range(edge, pairs - edge), sel, et, u)
+    filter_inner(d, u, a_bufs, pad, p0_out, 0)
     p = lax.broadcasted_iota(jnp.int32, (d.groups * 8, LANES), 0)
     cm[...] = jnp.where(p < D, hasw, jnp.where(p >= D + d.cols, hase, 1.0))
     low8 = lane_iota(8) < LANES // 2
@@ -432,6 +493,7 @@
         ref[0:BASE, :] = zero(BASE)
         ref[BASE + d.rr * d.st:d.size, :] = zero(8)
 
+    exchange_finish(d, gpairs, ex0, gcopies)
     for c in ecopies:
         c.wait_recv()
     low = lane_iota(d.cols) < LANES // 2
@@ -458,21 +520,28 @@
             et[row_at(j - D) + off:row_at(j - D) + off + 4, :] = nv[j * 4:j * 4 + 4, :]
             et[row_at(d.r + j) + off:row_at(d.r + j) + off + 4, :] = sv[j * 4:j * 4 + 4, :]
 
-    def g_step(g_o, g_r, po, out, n, yo, yr):
-        expand(d, g_o, g_r, sel, et, u)
-        half_filter(d, u, (a1, a2, a3), pad, po, masks)
-        copy = pltpu.make_async_copy(po, out, osem.at[n])
-        copy.start()
+    def g_rest(g_o, g_r, po, yo, yr, margin):
+        own, ring = wide(g_o), wide(g_r)
+        expand(d, ring, ring_pairs(edge), sel, et, u)
+        if margin:
+            expand(d, own, list(range(edge, 2 * edge)) + list(range(pairs - 2 * edge, pairs - edge)), sel, et, u)
+        first = edge + margin // 2
+        expand_edges(d, own, range(first, pairs - first), sel, et, u)
+        filter_outer(d, u, a_bufs, pad, po, margin, masks)
         back_filter(d, pad, (b1, b2, b3), et, lhs, masks)
         reduce_members(d, lhs, bsel, yo, yr)
-        return copy
-
-    o0 = g_step(go, gr, po0, p0_out, 0, y0o, y0r)
-    ycopies = exchange(d, [(y0o, y0r)], ex1)
+
+    g_rest(go, gr, p0_out, y0o, y0r, 0)
+    ycopies = exchange_start(d, [(y0o, y0r)], ex1)
+    g1o[...] = do[...] * y0o[...]
+    expand(d, wide(g1o), range(2 * edge, pairs - 2 * edge), sel, et, u)
+    filter_inner(d, u, a_bufs, pad, p1_out, D)
+    exchange_finish(d, [(y0o, y0r)], ex1, ycopies)
     g1o[...] = do[...] * y0o[...]
     g1r[...] = dr[...] * y0r[...]
-    o1 = g_step(g1o, g1r, po1, p1_out, 1, y1o, y1r)
-    zcopies = exchange(d, [(y1o, y1r)], ex2)
+    g_rest(g1o, g1r, p1_out, y1o, y1r, D)
+    zcopies = exchange_start(d, [(y1o, y1r)], ex2)
+    exchange_finish(d, [(y1o, y1r)], ex2, zcopies)
     inner = slice(D, D + d.cols)
     y0, y1, g0, g1, dd = y0o[inner, :], y1o[inner, :], go[inner, :], g1o[inner, :], do[inner, :]
     lane1 = lane_iota(1)
@@ -487,11 +556,9 @@
     ym_out[2 * d.cols:2 * d.cols + 8, :] = jnp.broadcast_to(total, (8, LANES))
     for c in ecopies + gcopies + ycopies + zcopies + scopies:
         c.wait_send()
-    o0.wait()
-    o1.wait()
-
-
-def final_kernel(d, p0, p1, ym, c_ref, inc_ref):
+
+
+def final_kernel(d, step, p0, p1, ym, c_ref, inc_ref, buf, sem):
     y0, y1, m = ym[0:d.cols], ym[d.cols:2 * d.cols], ym[2 * d.cols:2 * d.cols + 1]
     m = [m[:, k:k + 1] for k in range(4)]
     bn2 = m[0] + EPS
@@ -503,19 +570,33 @@
     alpha2 = (r2 + rho) / b2
     det = alpha1 * alpha2 - b2
     ca, cb = (alpha2 - c) / det, -1.0 / det
-    wide = lambda v: jnp.broadcast_to(v, (LANES, LANES))
+    full = lambda v: jnp.broadcast_to(v, (LANES, LANES))
     scale = KAPPA ** SWEEPS
-    sa, sb = wide(ca * scale), wide(cb * scale)
-    inc = (wide(ca) * y0 + wide(cb) * y1).T
+    sa, sb = full(ca * scale), full(cb * scale)
+
+    def copy(j):
+        return pltpu.make_async_copy(
+            buf.at[j].reshape(d.fields * d.halves, step, LANES),
+            c_ref.at[:, pl.ds(pl.multiple_of(j * step, step), step), :], sem.at[j])
+
+    def chunk(j, x):
+        for t in range(step):
+            r = j * step + t
+            v = (sa * p0[r] + sb * p1[r]).T
+            for h in range(d.halves):
+                for f in range(0, d.fields, 8):
+                    at = h * d.fields + f
+                    buf[j, pl.ds((f * d.halves + h) * step + t, 8, stride=d.halves * step), :] = v[at:at + 8]
+        copy(j).start()
+        return x
+
+    steps = d.r // step
+    lax.fori_loop(0, steps, chunk, 0)
+    inc = (full(ca) * y0 + full(cb) * y1).T
     for l in range(d.levels):
         inc_ref[l] = inc[l * d.rows:(l + 1) * d.rows]
-    step = p0.shape[0]
-    for r in range(step):
-        v = (sa * p0[r] + sb * p1[r]).T
-        for h in range(d.halves):
-            for f in range(0, d.fields, 8):
-                at = h * d.fields + f
-                c_ref[pl.ds((f * d.halves + h) * step + r, 8, stride=d.halves * step), :] = v[at:at + 8]
+    for j in range(steps):
+        copy(j).wait()
 
 
 def on_device(ensemble, obs_cell, obs_level, innovation, obs_weight):
@@ -530,7 +611,7 @@
     shape = lambda *s: jax.ShapeDtypeStruct(s, f32)
     scratch = [v(d.fields * (rows + 1), LANES)] + [v(d.size, LANES)] * 9
     scratch += [pltpu.VMEM((d.rr // 2, 256, 256), bf16), pltpu.VMEM((d.rr * 256, LANES), bf16),
-                pltpu.VMEM((d.st, d.rr * 256), bf16), v(d.r, cols, LANES), v(d.r, cols, LANES)]
+                pltpu.VMEM((d.st, d.rr * 256), bf16)]
     scratch += [v(d.groups * 8, LANES), v(8, LANES), v(8, LANES)]
     side = d.r * 4
     scratch += [v(2, cols, LANES), v(2, cols, LANES), v(side, LANES), v(side, LANES)] * 2
@@ -541,7 +622,7 @@
     obs = obs_cell.shape[-1]
     scratch += [v(1, LANES), v(n, 1, LANES), dma((n,)), dma((n,))]
     scratch += [pltpu.VMEM(ensemble.shape, bf16)] + [pltpu.VMEM((1, obs), jnp.int32)] * 2 + [v(1, obs)] * 2
-    scratch += [dma((8,)), dma((2,))]
+    scratch += [dma((8,))]
 
     def main_entry(*refs):
         main_kernel(d, *refs)
@@ -550,45 +631,24 @@
         main_entry,
         out_shape=(shape(d.r, cols, LANES), shape(d.r, cols, LANES), shape(2 * cols + 8, LANES)),
         in_specs=[hbm] * 5,
-        out_specs=(hbm, hbm, vm),
+        out_specs=(vm, vm, vm),
         scratch_shapes=scratch,
-        compiler_params=pltpu.CompilerParams(collective_id=0, has_side_effects=True, vmem_limit_bytes=64000000),
-    )(ensemble, flat(obs_cell), flat(obs_level), flat(innovation), flat(obs_weight))
+        compiler_params=pltpu.CompilerParams(collective_id=0, has_side_effects=True, vmem_limit_bytes=48000000),
+    )(*[pltpu.with_memory_space_constraint(a, pltpu.HBM) for a in (
+        ensemble, flat(obs_cell), flat(obs_level), flat(innovation), flat(obs_weight))])
     step = 8
     block = d.fields * d.halves * step
-    full = lambda *s: pl.BlockSpec(s, lambda i: (0,) * len(s))
-    out4 = (d.r // step, block, LANES)
-
-    def final_grid(p0, p1, ym, c_ref, inc_ref, buf, sem):
-        i = pl.program_id(0)
-        steps = pl.num_programs(0)
-        slot = lax.rem(i, 2)
-
-        def copy(j, k):
-            return pltpu.make_async_copy(
-                buf.at[k].reshape(d.fields * d.halves, step, LANES),
-                c_ref.at[:, pl.ds(pl.multiple_of(j * step, step), step), :], sem.at[k])
-
-        @pl.when(i >= 2)
-        def _():
-            copy(i - 2, slot).wait()
-
-        final_kernel(d, p0, p1, ym, buf.at[slot], inc_ref)
-        copy(i, slot).start()
-
-        @pl.when(i == steps - 1)
-        def _():
-            copy(i - 1, 1 - slot).wait()
-            copy(i, slot).wait()
+
+    def final_entry(*refs):
+        final_kernel(d, step, *refs)
 
     control, increment = pl.pallas_call(
-        final_grid,
-        grid=(d.r // step,),
+        final_entry,
         out_shape=(shape(d.fields * d.halves, d.r, LANES), shape(levels, rows, cols)),
-        in_specs=[pl.BlockSpec((step, cols, LANES), lambda i: (i, 0, 0))] * 2 + [full(2 * cols + 8, LANES)],
-        out_specs=(hbm, full(levels, rows, cols)),
-        scratch_shapes=[v(2, block, LANES), dma((2,))],
-        compiler_params=pltpu.CompilerParams(vmem_limit_bytes=64000000),
+        in_specs=[vm] * 3,
+        out_specs=(hbm, vm),
+        scratch_shapes=[v(d.r // step, block, LANES), dma((d.r // step,))],
+        compiler_params=pltpu.CompilerParams(vmem_limit_bytes=16000000),
     )(p0, p1, ym)
     return (control.reshape(members, levels, rows, cols), increment)
 

time: 50.5 us -> 43.4 us (0.86)
  Pallas kernels: 49.7 us -> 42.6 us
    pallas_call x1, Pallas kernels: 43.7 us -> 39.9 us  [on_device(): pl.pallas_call(main_entry, out_shape=(shape(d.r, cols, LANES), shape(d.r,...]
    pallas_call x1, Pallas kernels: 6.01 us -> 2.76 us  [on_device(): pl.pallas_call(final_entry, out_shape=(shape(d.fields * d.halves, d.r, LA...]
where the time goes in v3:
time: 43.4 us; the launch traced here: 43.3 us
  Pallas kernels  42.6 us (98%)
  between operations  0.64 us (1%)
    pallas_call x1, Pallas kernels, on_device(): pl.pallas_call(main_entry, out_shape=(shape(d.r, cols, LANES), shape(d.r,...  39.9 us
    pallas_call x1, Pallas kernels, on_device(): pl.pallas_call(final_entry, out_shape=(shape(d.fields * d.halves, d.r, LA...  2.76 us

profile of v3, /device:TPU:0, one launch (start us, length us, event | category | flops | bytes accessed | tf_op | source)
XLA Modules:
  0.0 43.3 jit_solution(3990699655999781258)
XLA Ops:
  0.6 39.9 %shard_map.68 = (f32[32,128,128]{2,1,0:T(8,128)S(1)}, f32[32,128,128]{2,1,0:T(8,128)S(1)}, f32[264,128]{1,0:T(8,128)S(1)}) custom-call(bf16[32,2,64,128]{3,2,1,0:T(8,128)(2,1)} %refs_0_.1, s32[1,2048]{1,0:T(1,128)} %bitcast.5, s32[1,2048]{1,0:T(1,128)} %bitcast.6, f32[1,2048]{1,0:T(1,128)} %bitcast.7, f32[1,2048]{1,0:T(1,128)} %bitcast.8), custom_call_target="tpu_custom_call" | custom-call | tf_op jit(solution)/shard_map/pallas_call | solution.py:630
  40.5 2.8 %shard_map.69 = (f32[128,32,128]{2,1,0:T(8,128)}, f32[2,64,128]{2,1,0:T(8,128)}) custom-call(f32[32,128,128]{2,1,0:T(8,128)S(1)} %get-tuple-element.7.refs_0_, f32[32,128,128]{2,1,0:T(8,128)S(1)} %get-tuple-element.8.refs_1_, f32[264,128]{1,0:T(8,128)S(1)} %get-tuple-element.9.refs_2_), custom_call_target="tpu_custom_call" | custom-call | tf_op jit(solution)/shard_map/pallas_call | solution.py:645

commit v4 on v3

--- a/solution.py
+++ b/solution.py
@@ -125,8 +125,8 @@
     return one + one + [dma((8,)), dma((8,))]
 
 
-def exchange_start(d, pairs, bufs):
-    out, land, ssem, rsem = bufs[:8], bufs[8:16], bufs[16], bufs[17]
+def exchange_pack(d, pairs, bufs):
+    out = bufs[:8]
     lo, hi, mid = row_masks(d, 8)
     last = d.groups - 1
     at = lambda g: slice(g * 8, g * 8 + 8)
@@ -151,7 +151,16 @@
         for k in range(2):
             for j in range(3):
                 out[k][a, j] = packs[k][j]
-    return [Side(n, out[n], land[BACK[n]], ssem, rsem) for n in (N_, S_, W_, E_, NW, NE, SW, SE)]
+
+
+def exchange_send(bufs):
+    out, land, ssem, rsem = bufs[:8], bufs[8:16], bufs[16], bufs[17]
+    return [Side(n, out[n], land[BACK[n]], ssem, rsem) for n in range(len(SIDES))]
+
+
+def exchange_start(d, pairs, bufs):
+    exchange_pack(d, pairs, bufs)
+    return exchange_send(bufs)
 
 
 def exchange_finish(d, pairs, bufs, copies):
@@ -181,25 +190,26 @@
 
 
 def build_selectors(d, sel, bsel):
-    def code(x_iota, l_iota):
+    def code(x_iota, l_iota, shift):
         level = x_iota // d.rows
         half = l_iota // d.fields
-        base = lax.rem(lax.rem(x_iota, d.rows) - d.r * half + d.rows, d.rows)
+        base = lax.rem(lax.rem(x_iota, d.rows) - d.r * half - shift + d.rows, d.rows)
         return jnp.where(lax.rem(l_iota, d.levels) == level, base, -1)
 
     a = lax.broadcasted_iota(jnp.int32, (LANES, LANES), 0)
     b = lax.broadcasted_iota(jnp.int32, (LANES, LANES), 1)
-    for_sel, for_bsel = code(a, b), code(b, a)
+    for_sel = code(a, b, 0)
+    for_bsel = code(b, a, lax.rem(a, d.fields) // (d.fields // 2))
 
     def fill(q, x):
+        want = lax.rem(q * 2 - D + d.rows, d.rows)
+        two = jnp.where(for_bsel == want, 1.0, 0.0).astype(bf16)
+        for k in range(2):
+            bsel[pl.ds(pl.multiple_of(q * 256 + k * LANES, LANES), LANES), :] = two
         for s in range(2):
-            i = q * 2 + s
-            want = lax.rem(i - D + d.rows, d.rows)
-            one = jnp.where(for_sel == want, 1.0, 0.0).astype(bf16)
-            two = jnp.where(for_bsel == want, 1.0, 0.0).astype(bf16)
+            one = jnp.where(for_sel == want + s, 1.0, 0.0).astype(bf16)
             for k in range(2):
                 sel[q, k * LANES:(k + 1) * LANES, s * LANES:(s + 1) * LANES] = one
-                bsel[pl.ds(pl.multiple_of(i * 256 + k * LANES, LANES), LANES), :] = two
         return x
 
     lax.fori_loop(0, d.rr // 2, fill, 0)
@@ -246,26 +256,34 @@
         n, c = c, s
 
 
-def sweep(d, src, dst, ext, masks):
-    cm, rt, rb = masks
-
-    def body(g, x):
-        p = pl.multiple_of(g * 8, 8)
-        m = cm[pl.ds(p, 8), :]
-        mt, mb = m * rt[...], m * rb[...]
-
-        def use(r, v):
-            dst[pl.ds(p + (BASE + (r + D) * d.st), 8), :] = v * (mt if r < 0 else mb if r >= d.r else m)
-
-        stencil(d, src, p, -ext, d.r + ext, use)
+def spread(n, rows, body):
+    k = min(n, 5, max(1, 80 // rows))
+
+    def step(i, x):
+        for t in range(k):
+            body(i * k + t)
         return x
 
-    lax.fori_loop(0, d.groups, body, 0)
+    if n > k:
+        lax.fori_loop(0, n // k, step, 0)
+        for t in range(n // k * k, n):
+            body(t)
+    else:
+        for t in range(n):
+            body(t)
+
+
+def aligned(x, n):
+    return x if isinstance(x, int) else pl.multiple_of(x, n)
+
+
+def count(ranges):
+    return sum(hi - lo for lo, hi in ranges)
 
 
 def sweep_part(d, src, dst, ranges, groups, masks):
-    def body(g, x):
-        p = pl.multiple_of(groups[0] * 8 + g * (groups[1] * 8), 8)
+    def body(g):
+        p = aligned(groups[0] * 8 + g * (groups[1] * 8), 8)
         if masks is not None:
             cm, rt, rb = masks
             m = cm[pl.ds(p, 8), :]
@@ -278,14 +296,13 @@
 
         for lo, hi in ranges:
             stencil(d, src, p, lo, hi, use)
-        return x
-
-    lax.fori_loop(0, groups[2], body, 0)
+
+    spread(groups[2], count(ranges), body)
 
 
 def last_part(d, src, pad, po, ranges, groups):
-    def body(g, x):
-        c = pl.multiple_of(groups[0] * 8 + g * (groups[1] * 8), 8)
+    def body(g):
+        c = aligned(groups[0] * 8 + g * (groups[1] * 8), 8)
 
         def use(r, v):
             pad[pl.ds(c + (D + BASE + (r + D) * d.st), 8), :] = v
@@ -293,9 +310,8 @@
 
         for lo, hi in ranges:
             stencil(d, src, c + D, lo, hi, use)
-        return x
-
-    lax.fori_loop(0, groups[2], body, 0)
+
+    spread(groups[2], count(ranges), body)
 
 
 def filter_inner(d, src, bufs, pad, po, margin):
@@ -323,18 +339,21 @@
 
 
 def back_filter(d, pad, bufs, et, lhs, masks):
-    b1, b2, b3 = bufs
-    sweep(d, pad, b1, 1, masks)
-    sweep(d, b1, b2, 2, masks)
-    sweep(d, b2, b3, 3, masks)
+    src = pad
+    for k, dst in enumerate(bufs):
+        sweep_part(d, src, dst, [(-k - 1, d.r + k + 1)], (0, 1, d.groups), masks)
+        src = dst
     zero = jnp.zeros((8, LANES), f32)
-
-    def pair(p, q, both):
+    first = lane_iota(8) % d.fields < d.fields // 2
+    quarter = d.fields // 2
+
+    def pair(p, both):
         def ld(r, o):
-            return b3[pl.ds(p + (BASE + (r + D) * d.st + o), 8), :]
+            return src[pl.ds(p + (BASE + (r + D) * d.st + o), 8), :]
 
         n = [None, None]
         c = [ld(-D, 0), ld(-D, 8) if both else None]
+        even = None
         for r in range(-D, d.r + D):
             ts = []
             for k in range(2 if both else 1):
@@ -348,37 +367,42 @@
                     v = v + n[k]
                 n[k], c[k] = c[k], s
                 ts.append(v * et[pl.ds(p + (BASE + (r + D) * d.st + o), 8), :])
+            if (r + D) % 2 == 0:
+                even = ts
+                continue
+            folded = [jnp.where(first, a, b) + jnp.where(first, pltpu.roll(a, LANES - quarter, 1), pltpu.roll(b, quarter, 1))
+                      for a, b in zip(even, ts)]
             if not both:
-                ts.append(zero)
-            hi, lo = split(jnp.concatenate(ts, axis=0))
-            at = (r + D) * 2 * LANES
-            lhs[pl.ds(q, 16), at:at + LANES] = hi
-            lhs[pl.ds(q, 16), at + LANES:at + 2 * LANES] = lo
+                folded.append(zero)
+            hi, lo = split(jnp.concatenate(folded, axis=0))
+            at = (r + D) // 2 * 2 * LANES
+            lhs[pl.ds(p, 16), at:at + LANES] = hi
+            lhs[pl.ds(p, 16), at + LANES:at + 2 * LANES] = lo
 
     def body(g, x):
-        p = pl.multiple_of(g * 16, 16)
-        pair(p, p, True)
+        pair(pl.multiple_of(g * 16, 16), True)
         return x
 
     lax.fori_loop(0, d.groups // 2, body, 0)
-    pair(d.groups // 2 * 16, d.groups // 2 * 16, False)
+    pair(d.groups // 2 * 16, False)
 
 
 def reduce_members(d, lhs, bsel, yo, yr):
-    k0, k1, k2 = D * 2 * LANES, (D + d.r) * 2 * LANES, d.rr * 2 * LANES
+    k0, k1, k2 = D * LANES, (D + d.r) * LANES, d.rr * LANES
     scale = KAPPA ** (2 * SWEEPS)
     dot = lambda a, b: jnp.dot(lhs[:, a:b], bsel[a:b, :], preferred_element_type=f32)
     yo[...] = dot(k0, k1) * scale
     yr[...] = (dot(0, k0) + dot(k1, k2)) * scale
 
 
-def all_sum(x_ref, land, ssem, rsem):
+def all_sum(x_ref, land, ssem, rsem, meanwhile):
     copies = []
     for k, (dy, dx) in enumerate(others()):
         copies.append(pltpu.make_async_remote_copy(
             src_ref=x_ref, dst_ref=land.at[k], send_sem=ssem.at[k], recv_sem=rsem.at[k],
             device_id=peer(dy, dx), device_id_type=MESH))
         copies[-1].start()
+    meanwhile()
     for c in copies:
         c.wait_recv()
     total = x_ref[...]
@@ -400,7 +424,7 @@
     refs = list(refs)
     take = lambda n: [refs.pop(0) for _ in range(n)]
     ec, et, u, a1, a2, a3, pad, b1, b2, b3 = take(10)
-    sel, bsel, lhs = take(3)
+    sel, bsel, lhs, po0, po1 = take(5)
     cm, rt, rb = masks = take(3)
     hn, hs, hw, he, ln, ls, lw, le, lnw, lne, lsw, lse, esem, rsem = take(14)
     go, gr, do, dr, g1o, g1r, y0o, y0r, y1o, y1r = take(10)
@@ -419,10 +443,17 @@
              for k in range(4)]
     small = [pltpu.make_async_copy(a, b, isem.at[4 + k])
              for k, (a, b) in enumerate(((cell_in, cell), (level_in, level), (inn_in, inn), (wt_in, wt)))]
-    for c in loads + small:
+    for c in small + loads:
         c.start()
     for n, refs_n in enumerate(((ln,), (ls,), (lw,), (le,), (lnw,), (lne,), (lsw,), (lse,))):
         clear_absent(n, refs_n + tuple(ex[8 + n] for ex in (ex0, ex1, ex2)))
+    for c in small:
+        c.wait()
+    scatter(d, cell, level, inn, wt, go, do)
+    gr[...] = jnp.zeros_like(gr)
+    dr[...] = jnp.zeros_like(dr)
+    gpairs = [(go, gr), (do, dr)]
+    exchange_pack(d, gpairs, ex0)
 
     def convert(k, x):
         for l in range(d.levels):
@@ -450,29 +481,32 @@
             hw[to, :] = et[pl.ds(at, 4), :]
             he[to, :] = et[pl.ds(at + d.cols - 4, 4), :]
 
-    lax.fori_loop(0, d.r // 4, lambda q, x: (transpose_four(q), x)[1], 0)
+    def transpose_edges(k, x):
+        transpose_four(k * (d.r // 4 - 1))
+        return x
+
+    def transpose_two(k, x):
+        transpose_four(k * 2 + 1)
+        transpose_four(k * 2 + 2)
+        return x
+
+    lax.fori_loop(0, 2, transpose_edges, 0)
     ens_send_rows(d, et, hn, hs)
     n4 = d.r * 4
     meet_wait()
-    ecopies = [Side(N_, hn, ls, esem, rsem), Side(S_, hs, ln, esem, rsem),
-               Side(W_, hw, le, esem, rsem), Side(E_, he, lw, esem, rsem),
-               Side(NW, hw.at[0:16], lse, esem, rsem), Side(NE, he.at[0:16], lsw, esem, rsem),
-               Side(SW, hw.at[n4 - 16:n4], lne, esem, rsem), Side(SE, he.at[n4 - 16:n4], lnw, esem, rsem)]
-    for c in small:
-        c.wait()
-
-    scatter(d, cell, level, inn, wt, go, do)
-    gr[...] = jnp.zeros_like(gr)
-    dr[...] = jnp.zeros_like(dr)
-    gpairs = [(go, gr), (do, dr)]
-    gcopies = exchange_start(d, gpairs, ex0)
+    gcopies = exchange_send(ex0)
+    ecopies = [Side(N_, hn, ls, esem, rsem), Side(S_, hs, ln, esem, rsem)]
+    lax.fori_loop(0, d.r // 8 - 1, transpose_two, 0)
+    ecopies += [Side(W_, hw, le, esem, rsem), Side(E_, he, lw, esem, rsem),
+                Side(NW, hw.at[0:16], lse, esem, rsem), Side(NE, he.at[0:16], lsw, esem, rsem),
+                Side(SW, hw.at[n4 - 16:n4], lne, esem, rsem), Side(SE, he.at[n4 - 16:n4], lnw, esem, rsem)]
     build_selectors(d, sel, bsel)
     edge = D // 2
     pairs = d.rr // 2
     ring_pairs = lambda n: list(range(n)) + list(range(pairs - n, pairs))
     a_bufs = (a1, a2, a3)
     expand(d, wide(go), range(edge, pairs - edge), sel, et, u)
-    filter_inner(d, u, a_bufs, pad, p0_out, 0)
+    filter_inner(d, u, a_bufs, pad, po0, 0)
     p = lax.broadcasted_iota(jnp.int32, (d.groups * 8, LANES), 0)
     cm[...] = jnp.where(p < D, hasw, jnp.where(p >= D + d.cols, hase, 1.0))
     low8 = lane_iota(8) < LANES // 2
@@ -531,15 +565,15 @@
         back_filter(d, pad, (b1, b2, b3), et, lhs, masks)
         reduce_members(d, lhs, bsel, yo, yr)
 
-    g_rest(go, gr, p0_out, y0o, y0r, 0)
+    g_rest(go, gr, po0, y0o, y0r, 0)
     ycopies = exchange_start(d, [(y0o, y0r)], ex1)
     g1o[...] = do[...] * y0o[...]
     expand(d, wide(g1o), range(2 * edge, pairs - 2 * edge), sel, et, u)
-    filter_inner(d, u, a_bufs, pad, p1_out, D)
+    filter_inner(d, u, a_bufs, pad, po1, D)
     exchange_finish(d, [(y0o, y0r)], ex1, ycopies)
     g1o[...] = do[...] * y0o[...]
     g1r[...] = dr[...] * y0r[...]
-    g_rest(g1o, g1r, p1_out, y1o, y1r, D)
+    g_rest(g1o, g1r, po1, y1o, y1r, D)
     zcopies = exchange_start(d, [(y1o, y1r)], ex2)
     exchange_finish(d, [(y1o, y1r)], ex2, zcopies)
     inner = slice(D, D + d.cols)
@@ -550,16 +584,32 @@
         t = jnp.sum(jnp.sum(v, axis=0, keepdims=True), axis=1, keepdims=True)
         x = jnp.where(lane1 == k, t, x)
     x_ref[...] = x
-    ym_out[0:d.cols, :] = y0
-    ym_out[d.cols:2 * d.cols, :] = y1
-    scopies, total = all_sum(x_ref, sum_land, sum_s, sum_r)
+
+    def meanwhile():
+        ym_out[0:d.cols, :] = y0.T
+        ym_out[d.cols:2 * d.cols, :] = y1.T
+
+        def body(q, x):
+            for po, out in ((po0, p0_out), (po1, p1_out)):
+                for t in range(2):
+                    r = q * 2 + t
+                    v = po[r].T
+                    for h in range(d.halves):
+                        for f in range(0, d.fields, 8):
+                            at = h * d.fields + f
+                            out[pl.ds(f * d.rows + h * d.r + r, 8, stride=d.rows), :] = v[at:at + 8]
+            return x
+
+        lax.fori_loop(0, d.r // 2, body, 0)
+
+    scopies, total = all_sum(x_ref, sum_land, sum_s, sum_r, meanwhile)
     ym_out[2 * d.cols:2 * d.cols + 8, :] = jnp.broadcast_to(total, (8, LANES))
     for c in ecopies + gcopies + ycopies + zcopies + scopies:
         c.wait_send()
 
 
-def final_kernel(d, step, p0, p1, ym, c_ref, inc_ref, buf, sem):
-    y0, y1, m = ym[0:d.cols], ym[d.cols:2 * d.cols], ym[2 * d.cols:2 * d.cols + 1]
+def final_kernel(d, steps, p0, p1, ym, c_ref, inc_ref, buf, sem):
+    m = ym[2 * d.cols:2 * d.cols + 1]
     m = [m[:, k:k + 1] for k in range(4)]
     bn2 = m[0] + EPS
     c = (EPS - m[1]) / bn2
@@ -570,31 +620,31 @@
     alpha2 = (r2 + rho) / b2
     det = alpha1 * alpha2 - b2
     ca, cb = (alpha2 - c) / det, -1.0 / det
-    full = lambda v: jnp.broadcast_to(v, (LANES, LANES))
     scale = KAPPA ** SWEEPS
-    sa, sb = full(ca * scale), full(cb * scale)
+    full = lambda v: jnp.broadcast_to(v, (8, LANES))
+    sa, sb, ya, yb = full(ca * scale), full(cb * scale), full(ca), full(cb)
+    size = c_ref.shape[0] // steps
 
     def copy(j):
-        return pltpu.make_async_copy(
-            buf.at[j].reshape(d.fields * d.halves, step, LANES),
-            c_ref.at[:, pl.ds(pl.multiple_of(j * step, step), step), :], sem.at[j])
+        at = pl.ds(pl.multiple_of(j * size, size), size)
+        return pltpu.make_async_copy(buf.at[at], c_ref.at[at], sem.at[j])
 
     def chunk(j, x):
-        for t in range(step):
-            r = j * step + t
-            v = (sa * p0[r] + sb * p1[r]).T
-            for h in range(d.halves):
-                for f in range(0, d.fields, 8):
-                    at = h * d.fields + f
-                    buf[j, pl.ds((f * d.halves + h) * step + t, 8, stride=d.halves * step), :] = v[at:at + 8]
+        def some(i, x):
+            for t in range(16):
+                at = pl.ds(pl.multiple_of(j * size + i * 128 + t * 8, 8), 8)
+                buf[at, :] = sa * p0[at, :] + sb * p1[at, :]
+            return x
+
+        lax.fori_loop(0, size // 128, some, 0)
         copy(j).start()
         return x
 
-    steps = d.r // step
     lax.fori_loop(0, steps, chunk, 0)
-    inc = (full(ca) * y0 + full(cb) * y1).T
     for l in range(d.levels):
-        inc_ref[l] = inc[l * d.rows:(l + 1) * d.rows]
+        for t in range(0, d.rows, 8):
+            at = l * d.rows + t
+            inc_ref[l, t:t + 8] = ya * ym[at:at + 8] + yb * ym[d.cols + at:d.cols + at + 8]
     for j in range(steps):
         copy(j).wait()
 
@@ -610,8 +660,8 @@
     flat = lambda a: a.reshape(1, -1)
     shape = lambda *s: jax.ShapeDtypeStruct(s, f32)
     scratch = [v(d.fields * (rows + 1), LANES)] + [v(d.size, LANES)] * 9
-    scratch += [pltpu.VMEM((d.rr // 2, 256, 256), bf16), pltpu.VMEM((d.rr * 256, LANES), bf16),
-                pltpu.VMEM((d.st, d.rr * 256), bf16)]
+    scratch += [pltpu.VMEM((d.rr // 2, 256, 256), bf16), pltpu.VMEM((d.rr * LANES, LANES), bf16),
+                pltpu.VMEM((d.st, d.rr * LANES), bf16), v(d.r, cols, LANES), v(d.r, cols, LANES)]
     scratch += [v(d.groups * 8, LANES), v(8, LANES), v(8, LANES)]
     side = d.r * 4
     scratch += [v(2, cols, LANES), v(2, cols, LANES), v(side, LANES), v(side, LANES)] * 2
@@ -629,26 +679,25 @@
 
     p0, p1, ym = pl.pallas_call(
         main_entry,
-        out_shape=(shape(d.r, cols, LANES), shape(d.r, cols, LANES), shape(2 * cols + 8, LANES)),
+        out_shape=(shape(d.fields * rows, cols), shape(d.fields * rows, cols), shape(2 * cols + 8, LANES)),
         in_specs=[hbm] * 5,
         out_specs=(vm, vm, vm),
         scratch_shapes=scratch,
         compiler_params=pltpu.CompilerParams(collective_id=0, has_side_effects=True, vmem_limit_bytes=48000000),
     )(*[pltpu.with_memory_space_constraint(a, pltpu.HBM) for a in (
         ensemble, flat(obs_cell), flat(obs_level), flat(innovation), flat(obs_weight))])
-    step = 8
-    block = d.fields * d.halves * step
+    steps = 8
 
     def final_entry(*refs):
-        final_kernel(d, step, *refs)
+        final_kernel(d, steps, *refs)
 
     control, increment = pl.pallas_call(
         final_entry,
-        out_shape=(shape(d.fields * d.halves, d.r, LANES), shape(levels, rows, cols)),
+        out_shape=(shape(d.fields * rows, cols), shape(levels, rows, cols)),
         in_specs=[vm] * 3,
         out_specs=(hbm, vm),
-        scratch_shapes=[v(d.r // step, block, LANES), dma((d.r // step,))],
-        compiler_params=pltpu.CompilerParams(vmem_limit_bytes=16000000),
+        scratch_shapes=[v(d.fields * rows, cols), dma((steps,))],
+        compiler_params=pltpu.CompilerParams(vmem_limit_bytes=8000000),
     )(p0, p1, ym)
     return (control.reshape(members, levels, rows, cols), increment)
 

time: 43.4 us -> 41.9 us (0.965)
  Pallas kernels: 42.6 us -> 41 us
    pallas_call x2, Pallas kernels: 42.6 us -> 41 us  [the longest x1 38.6 us: on_device(): pl.pallas_call(main_entry, out_shape=(shape(d.fields * rows, cols), shape...]
where the time goes in v4:
time: 41.9 us; the launch traced here: 41.6 us
  Pallas kernels  41 us (98%)
  between operations  0.64 us (2%)
    pallas_call x1, Pallas kernels, on_device(): pl.pallas_call(main_entry, out_shape=(shape(d.fields * rows, cols), shape...  38.6 us
    pallas_call x1, Pallas kernels, on_device(): pl.pallas_call(final_entry, out_shape=(shape(d.fields * rows, cols), shap...  2.39 us

profile of v4, /device:TPU:0, one launch (start us, length us, event | category | flops | bytes accessed | tf_op | source)
XLA Modules:
  0.0 41.6 jit_solution(13567367227724796501)
XLA Ops:
  0.6 38.6 %shard_map.68 = (f32[4096,128]{1,0:T(8,128)S(1)}, f32[4096,128]{1,0:T(8,128)S(1)}, f32[264,128]{1,0:T(8,128)S(1)}) custom-call(bf16[32,2,64,128]{3,2,1,0:T(8,128)(2,1)} %refs_0_.1, s32[1,2048]{1,0:T(1,128)} %bitcast.5, s32[1,2048]{1,0:T(1,128)} %bitcast.6, f32[1,2048]{1,0:T(1,128)} %bitcast.7, f32[1,2048]{1,0:T(1,128)} %bitcast.8), custom_call_target="tpu_custom_call" | custom-call | tf_op jit(solution)/shard_map/pallas_call | solution.py:680
  39.3 2.4 %shard_map.69 = (f32[4096,128]{1,0:T(8,128)}, f32[2,64,128]{2,1,0:T(8,128)}) custom-call(f32[4096,128]{1,0:T(8,128)S(1)} %get-tuple-element.7.refs_0_, f32[4096,128]{1,0:T(8,128)S(1)} %get-tuple-element.8.refs_1_, f32[264,128]{1,0:T(8,128)S(1)} %get-tuple-element.9.refs_2_), custom_call_target="tpu_custom_call" | custom-call | tf_op jit(solution)/shard_map/pallas_call | solution.py:694

commit v5 on v4

--- a/solution.py
+++ b/solution.py
@@ -338,32 +338,28 @@
     last_part(d, src, pad, po, [(0, d.r)], (0, n - 1, 2))
 
 
-def back_filter(d, pad, bufs, et, lhs, masks):
-    src = pad
-    for k, dst in enumerate(bufs):
-        sweep_part(d, src, dst, [(-k - 1, d.r + k + 1)], (0, 1, d.groups), masks)
-        src = dst
-    zero = jnp.zeros((8, LANES), f32)
+def spread_back(d, src, et, lhs, p, both, ranges):
     first = lane_iota(8) % d.fields < d.fields // 2
     quarter = d.fields // 2
-
-    def pair(p, both):
-        def ld(r, o):
-            return src[pl.ds(p + (BASE + (r + D) * d.st + o), 8), :]
-
-        n = [None, None]
-        c = [ld(-D, 0), ld(-D, 8) if both else None]
+    keys = range(2 if both else 1)
+
+    def ld(r, o):
+        return src[pl.ds(p + (BASE + (r + D) * d.st + o), 8), :]
+
+    for lo, hi in ranges:
+        n = [ld(lo - 1, 8 * k) if lo > -D else None for k in keys]
+        c = [ld(lo, 8 * k) for k in keys]
         even = None
-        for r in range(-D, d.r + D):
+        for r in range(lo, hi):
             ts = []
-            for k in range(2 if both else 1):
+            for k in keys:
                 o = 8 * k
                 v = c[k] + (ld(r, o - 1) + ld(r, o + 1))
                 s = None
                 if r < d.r + D - 1:
                     s = ld(r + 1, o)
                     v = v + s
-                if r > -D:
+                if n[k] is not None:
                     v = v + n[k]
                 n[k], c[k] = c[k], s
                 ts.append(v * et[pl.ds(p + (BASE + (r + D) * d.st + o), 8), :])
@@ -373,18 +369,50 @@
             folded = [jnp.where(first, a, b) + jnp.where(first, pltpu.roll(a, LANES - quarter, 1), pltpu.roll(b, quarter, 1))
                       for a, b in zip(even, ts)]
             if not both:
-                folded.append(zero)
-            hi, lo = split(jnp.concatenate(folded, axis=0))
+                folded.append(jnp.zeros((8, LANES), f32))
+            up, down = split(jnp.concatenate(folded, axis=0))
             at = (r + D) // 2 * 2 * LANES
-            lhs[pl.ds(p, 16), at:at + LANES] = hi
-            lhs[pl.ds(p, 16), at + LANES:at + 2 * LANES] = lo
-
+            lhs[pl.ds(p, 16), at:at + LANES] = up
+            lhs[pl.ds(p, 16), at + LANES:at + 2 * LANES] = down
+
+
+def back_pairs(d, src, et, lhs, start, n, ranges):
     def body(g, x):
-        pair(pl.multiple_of(g * 16, 16), True)
+        spread_back(d, src, et, lhs, pl.multiple_of((start + g) * 16, 16), True, ranges)
         return x
 
-    lax.fori_loop(0, d.groups // 2, body, 0)
-    pair(d.groups // 2 * 16, False)
+    lax.fori_loop(0, n, body, 0)
+
+
+def back_inner(d, pad, bufs, et, lhs):
+    src = pad
+    for k, dst in enumerate(bufs):
+        m = D + k + 1
+        sweep_part(d, src, dst, [(m, d.r - m)], (1, 1, d.groups - 2), None)
+        src = dst
+    back_pairs(d, src, et, lhs, 1, d.groups // 2 - 2, [(2 * D, d.r - 2 * D)])
+
+
+def back_filter(d, pad, bufs, et, lhs, masks, inner_done):
+    src = pad
+    for k, dst in enumerate(bufs):
+        e, m = k + 1, D + k + 1
+        if inner_done:
+            sweep_part(d, src, dst, [(-e, m), (d.r - m, d.r + e)], (2, 1, d.groups - 4), masks)
+            for t in range(2):
+                sweep_part(d, src, dst, [(-e, d.r + e)], (t, d.groups - 2, 2), masks)
+        else:
+            sweep_part(d, src, dst, [(-e, d.r + e)], (0, 1, d.groups), masks)
+        src = dst
+    rows = [(-D, d.r + D)]
+    n = d.groups // 2
+    if inner_done:
+        back_pairs(d, src, et, lhs, 1, n - 2, [(-D, 2 * D), (d.r - 2 * D, d.r + D)])
+        for q in (0, n - 1):
+            spread_back(d, src, et, lhs, q * 16, True, rows)
+    else:
+        back_pairs(d, src, et, lhs, 0, n, rows)
+    spread_back(d, src, et, lhs, n * 16, False, rows)
 
 
 def reduce_members(d, lhs, bsel, yo, yr):
@@ -428,7 +456,7 @@
     cm, rt, rb = masks = take(3)
     hn, hs, hw, he, ln, ls, lw, le, lnw, lne, lsw, lse, esem, rsem = take(14)
     go, gr, do, dr, g1o, g1r, y0o, y0r, y1o, y1r = take(10)
-    ex0, ex1, ex2 = take(18), take(18), take(18)
+    ex0, exd, ex1, ex2 = take(18), take(18), take(18), take(18)
     x_ref, sum_land, sum_s, sum_r = take(4)
     ens, cell, level, inn, wt, isem = take(6)
     es = d.rows + 1
@@ -446,14 +474,15 @@
     for c in small + loads:
         c.start()
     for n, refs_n in enumerate(((ln,), (ls,), (lw,), (le,), (lnw,), (lne,), (lsw,), (lse,))):
-        clear_absent(n, refs_n + tuple(ex[8 + n] for ex in (ex0, ex1, ex2)))
+        clear_absent(n, refs_n + tuple(ex[8 + n] for ex in (ex0, exd, ex1, ex2)))
     for c in small:
         c.wait()
     scatter(d, cell, level, inn, wt, go, do)
     gr[...] = jnp.zeros_like(gr)
     dr[...] = jnp.zeros_like(dr)
-    gpairs = [(go, gr), (do, dr)]
+    gpairs, dpairs = [(go, gr)], [(do, dr)]
     exchange_pack(d, gpairs, ex0)
+    exchange_pack(d, dpairs, exd)
 
     def convert(k, x):
         for l in range(d.levels):
@@ -500,6 +529,7 @@
     ecopies += [Side(W_, hw, le, esem, rsem), Side(E_, he, lw, esem, rsem),
                 Side(NW, hw.at[0:16], lse, esem, rsem), Side(NE, he.at[0:16], lsw, esem, rsem),
                 Side(SW, hw.at[n4 - 16:n4], lne, esem, rsem), Side(SE, he.at[n4 - 16:n4], lnw, esem, rsem)]
+    dcopies = exchange_send(exd)
     build_selectors(d, sel, bsel)
     edge = D // 2
     pairs = d.rr // 2
@@ -507,6 +537,7 @@
     a_bufs = (a1, a2, a3)
     expand(d, wide(go), range(edge, pairs - edge), sel, et, u)
     filter_inner(d, u, a_bufs, pad, po0, 0)
+    back_inner(d, pad, (b1, b2, b3), et, lhs)
     p = lax.broadcasted_iota(jnp.int32, (d.groups * 8, LANES), 0)
     cm[...] = jnp.where(p < D, hasw, jnp.where(p >= D + d.cols, hase, 1.0))
     low8 = lane_iota(8) < LANES // 2
@@ -562,7 +593,7 @@
         first = edge + margin // 2
         expand_edges(d, own, range(first, pairs - first), sel, et, u)
         filter_outer(d, u, a_bufs, pad, po, margin, masks)
-        back_filter(d, pad, (b1, b2, b3), et, lhs, masks)
+        back_filter(d, pad, (b1, b2, b3), et, lhs, masks, margin == 0)
         reduce_members(d, lhs, bsel, yo, yr)
 
     g_rest(go, gr, po0, y0o, y0r, 0)
@@ -570,6 +601,7 @@
     g1o[...] = do[...] * y0o[...]
     expand(d, wide(g1o), range(2 * edge, pairs - 2 * edge), sel, et, u)
     filter_inner(d, u, a_bufs, pad, po1, D)
+    exchange_finish(d, dpairs, exd, dcopies)
     exchange_finish(d, [(y0o, y0r)], ex1, ycopies)
     g1o[...] = do[...] * y0o[...]
     g1r[...] = dr[...] * y0r[...]
@@ -604,7 +636,7 @@
 
     scopies, total = all_sum(x_ref, sum_land, sum_s, sum_r, meanwhile)
     ym_out[2 * d.cols:2 * d.cols + 8, :] = jnp.broadcast_to(total, (8, LANES))
-    for c in ecopies + gcopies + ycopies + zcopies + scopies:
+    for c in ecopies + gcopies + dcopies + ycopies + zcopies + scopies:
         c.wait_send()
 
 
@@ -667,7 +699,7 @@
     scratch += [v(2, cols, LANES), v(2, cols, LANES), v(side, LANES), v(side, LANES)] * 2
     scratch += [v(16, LANES)] * 4 + [dma((8,)), dma((8,))]
     scratch += [v(d.st, LANES)] * 10
-    scratch += exchange_buffers(2) + exchange_buffers(1) + exchange_buffers(1)
+    scratch += exchange_buffers(1) * 4
     n = nx * ny - 1
     obs = obs_cell.shape[-1]
     scratch += [v(1, LANES), v(n, 1, LANES), dma((n,)), dma((n,))]

time: 41.9 us -> 40.4 us (0.964)
  Pallas kernels: 41 us -> 39.6 us
    pallas_call x1, Pallas kernels: 38.6 us -> 37.2 us  [on_device(): pl.pallas_call(main_entry, out_shape=(shape(d.fields * rows, cols), shape...]
where the time goes in v5:
time: 40.4 us; the launch traced here: 40.2 us
  Pallas kernels  39.6 us (98%)
  between operations  0.64 us (2%)
    pallas_call x1, Pallas kernels, on_device(): pl.pallas_call(main_entry, out_shape=(shape(d.fields * rows, cols), shape...  37.2 us
    pallas_call x1, Pallas kernels, on_device(): pl.pallas_call(final_entry, out_shape=(shape(d.fields * rows, cols), shap...  2.39 us

profile of v5, /device:TPU:0, one launch (start us, length us, event | category | flops | bytes accessed | tf_op | source)
XLA Modules:
  0.0 40.2 jit_solution(4883105326281274594)
XLA Ops:
  0.6 37.2 %shard_map.68 = (f32[4096,128]{1,0:T(8,128)S(1)}, f32[4096,128]{1,0:T(8,128)S(1)}, f32[264,128]{1,0:T(8,128)S(1)}) custom-call(bf16[32,2,64,128]{3,2,1,0:T(8,128)(2,1)} %refs_0_.1, s32[1,2048]{1,0:T(1,128)} %bitcast.5, s32[1,2048]{1,0:T(1,128)} %bitcast.6, f32[1,2048]{1,0:T(1,128)} %bitcast.7, f32[1,2048]{1,0:T(1,128)} %bitcast.8), custom_call_target="tpu_custom_call" | custom-call | tf_op jit(solution)/shard_map/pallas_call | solution.py:712
  37.8 2.4 %shard_map.69 = (f32[4096,128]{1,0:T(8,128)}, f32[2,64,128]{2,1,0:T(8,128)}) custom-call(f32[4096,128]{1,0:T(8,128)S(1)} %get-tuple-element.7.refs_0_, f32[4096,128]{1,0:T(8,128)S(1)} %get-tuple-element.8.refs_1_, f32[264,128]{1,0:T(8,128)S(1)} %get-tuple-element.9.refs_2_), custom_call_target="tpu_custom_call" | custom-call | tf_op jit(solution)/shard_map/pallas_call | solution.py:726
